TPU v7x, 256 devices: a whole 4x4x8 slice. The times are simulated.
256 devices in a mesh: band: 64 (over x, z, y_hi), img: 4 (over y_lo, core).
Axes of the slice: x: 4, y: 4 (y_hi: 2, y_lo: 2; y = y_hi * 2 + y_lo), z: 8, core: 2. Of those that a mesh axis runs over, the one named last changes fastest.
Arguments:
- pixels: bfloat16 [2048, 256, 180], P(('img', 'band')), parts along dimension 0, may hold values from -12 to 12
- keep_mask: int32 [256, 32], P(('img', 'band')), parts along dimension 0, may hold values from 0 to 1, as said below
- band_counts: int32 [256], P(('img', 'band')), parts along dimension 0, may hold values from 0 to 32, as said below
- plan_dest: int32 [256, 16], P(('img', 'band')), parts along dimension 0, may hold values from 0 to 63, as said below
- plan_slot: int32 [256, 16], P(('img', 'band')), parts along dimension 0, may hold values from 0 to 8, as said below
- bias_table: float32 [225, 6], replicated, may hold values from -4 to 4
- gain_attn: float32 [180], replicated, may hold values from 0.25 to 1.75
- qkv_weight: bfloat16 [180, 540], replicated, may hold values from -5 to 5
- proj_weight: bfloat16 [180, 180], replicated, may hold values from -0.4375 to 0.4375
- gain_mlp: float32 [180], replicated, may hold values from 0.25 to 1.75
- hidden_weight: bfloat16 [180, 360], replicated, may hold values from -0.4375 to 0.4375
- output_weight: bfloat16 [360, 180], replicated, may hold values from -0.3125 to 0.3125
Outputs:
- restored: bfloat16 [2048, 256, 180], P(('img', 'band')), parts along dimension 0
- work_tiles: bfloat16 [2048, 128, 180], P(('img', 'band')), parts along dimension 0
There are 4 independent parts, one for each index of `img`. A program takes and returns all parts, laid end to end along the dimension named above; an argument that names none is the same for every part. Nothing has to cross between parts.
Inputs may be any that keep to these rules, and one draw needn't show every extreme that they name: `keep_mask`: the number of ones in a band varies strongly from band to band. band_counts[b] equals the number of ones among band b's windows in keep_mask. A band's live tiles are those with 2 t < band_counts[b]; their number summed over bands lies between 449 and 512, and some band has all 16 tiles live. `plan_dest`: within each aligned group of 64 consecutive tiles of a band (equal t // 64) the destinations are all different. `plan_slot`: 8 for tiles that are not live; a live tile has a slot below 8, no two live tiles of the image share destination and slot, and some destination receives 8 live tiles.
All inputs are finite; a program needn't handle non-finite values.
Results may differ from a plain program's by a relative error of at most 0.0044.
Values may be sent and summed in bfloat16 or wider, within the bound.
A program may use at most 64 MiB of HBM per device.

v0:
```python
import jax
import jax.numpy as jnp
from jax import lax
from jax.sharding import PartitionSpec as P

CHAN = 180
HEADS = 6
WIN = 8
TILE = 2
SHIFT = 4
CAP = 8


EPSILON = 1e-05


def from_behind(value, axis, steps):
    count = lax.axis_size(axis)
    pairs = [(source, (source + steps) % count) for source in range(count)]
    return lax.ppermute(value, axis, pairs)


def layer_norm(values, gain_vec):
    values = values.astype(jnp.float32)
    center = values - jnp.mean(values, axis=-1, keepdims=True)
    spread = jnp.mean(center * center, axis=-1, keepdims=True)
    return center * lax.rsqrt(spread + EPSILON) * gain_vec


def position_bias(bias_table):
    coords = jnp.arange(WIN * WIN, dtype=jnp.int32)
    row_pos = coords // WIN
    col_pos = coords % WIN
    table_index = (row_pos[:, None] - row_pos[None, :] + WIN - 1) * (2 * WIN - 1) + (
        col_pos[:, None] - col_pos[None, :] + WIN - 1
    )
    entries = bias_table.shape[0]
    onehot = (table_index.reshape(-1, 1) == jnp.arange(entries, dtype=jnp.int32)[None, :]).astype(
        jnp.float32
    )
    looked = jnp.dot(onehot, bias_table, precision=lax.Precision.HIGHEST)
    return jnp.transpose(looked.reshape(WIN * WIN, WIN * WIN, -1), (2, 0, 1))


def region_codes(first_row, row_count, height, col_count):
    rows_global = first_row + jnp.arange(row_count, dtype=jnp.int32)
    row_region = (rows_global >= height - WIN).astype(jnp.int32) + (
        rows_global >= height - SHIFT
    ).astype(jnp.int32)
    col_global = jnp.arange(col_count, dtype=jnp.int32)
    col_region = (col_global >= col_count - WIN).astype(jnp.int32) + (
        col_global >= col_count - SHIFT
    ).astype(jnp.int32)
    return 3 * row_region[:, None] + col_region[None, :]


def attend(windows, window_codes, head_bias, gain_attn, qkv_weight, proj_weight):
    window_count = windows.shape[0]
    head_dim = CHAN // HEADS
    normed = layer_norm(windows, gain_attn).astype(jnp.bfloat16).reshape(-1, CHAN)
    mixed_all = jnp.dot(normed, qkv_weight, preferred_element_type=jnp.float32).reshape(
        window_count, WIN * WIN, 3, HEADS, head_dim
    )
    queries = mixed_all[:, :, 0] * head_dim ** (-0.5)
    key_part = mixed_all[:, :, 1]
    value_part = mixed_all[:, :, 2].astype(jnp.bfloat16)
    scores = jnp.einsum("wqhd,wkhd->whqk", queries, key_part, precision=lax.Precision.HIGHEST)
    differ = window_codes[:, :, None] != window_codes[:, None, :]
    scores = scores + head_bias[None] + jnp.where(differ, -100.0, 0.0)[:, None]
    weights = jax.nn.softmax(scores, axis=-1).astype(jnp.bfloat16)
    mixed = jnp.einsum("whqk,wkhd->wqhd", weights, value_part, preferred_element_type=jnp.float32)
    mixed = mixed.reshape(-1, CHAN).astype(jnp.bfloat16)
    projected = jnp.dot(mixed, proj_weight, preferred_element_type=jnp.float32)
    summed = windows.reshape(-1, CHAN).astype(jnp.float32) + projected
    return summed.astype(jnp.bfloat16).reshape(window_count, WIN * WIN, CHAN)


def feed(states, gain_mlp, hidden_weight, output_weight):
    flat_rows = states.reshape(-1, CHAN)
    normed = layer_norm(flat_rows, gain_mlp).astype(jnp.bfloat16)
    inner_act = jax.nn.gelu(
        jnp.dot(normed, hidden_weight, preferred_element_type=jnp.float32)
    ).astype(jnp.bfloat16)
    summed = flat_rows.astype(jnp.float32) + jnp.dot(
        inner_act, output_weight, preferred_element_type=jnp.float32
    )
    return summed.astype(jnp.bfloat16).reshape(states.shape)


def shards(
    pixels,
    keep_mask,
    band_counts,
    plan_dest,
    plan_slot,
    bias_table,
    gain_attn,
    qkv_weight,
    proj_weight,
    gain_mlp,
    hidden_weight,
    output_weight,
):
    band_total = lax.axis_size("band")
    band_index = lax.axis_index("band")
    row_count, col_count, channels = pixels.shape
    win_rows = row_count // WIN
    win_cols = col_count // WIN
    window_total = win_rows * win_cols
    tile_total = window_total // TILE
    tile_tokens = TILE * WIN * WIN
    pair_slots = -(-tile_total // band_total)
    lower_rows = from_behind(pixels[:SHIFT], "band", -1)
    shifted = jnp.roll(jnp.concatenate([pixels[SHIFT:], lower_rows], axis=0), -SHIFT, axis=1)
    windows = (
        shifted.reshape(win_rows, WIN, win_cols, WIN, channels)
        .transpose(0, 2, 1, 3, 4)
        .reshape(window_total, WIN * WIN, channels)
    )
    region_map = region_codes(band_index * row_count, row_count, band_total * row_count, col_count)
    window_codes = (
        region_map.reshape(win_rows, WIN, win_cols, WIN)
        .transpose(0, 2, 1, 3)
        .reshape(window_total, WIN * WIN)
    )
    band_keep = keep_mask.reshape(window_total)
    kept_count = band_counts[0]
    packed_order = jnp.cumsum(band_keep) - 1
    active = (band_keep == 1) & (packed_order < kept_count)
    target = jnp.where(active, packed_order, window_total)
    packed = (
        jnp.zeros((window_total + 1, WIN * WIN, channels), jnp.bfloat16)
        .at[target]
        .set(windows)[:window_total]
    )
    packed_codes = (
        jnp.zeros((window_total + 1, WIN * WIN), jnp.bfloat16)
        .at[target]
        .set(window_codes.astype(jnp.bfloat16))[:window_total]
    )
    tile_ids = jnp.arange(tile_total, dtype=jnp.int32)
    tile_live = tile_ids * TILE < kept_count
    destinations = plan_dest[0]
    pair_index = tile_ids // band_total
    sent_slot = jnp.where(tile_live, plan_slot[0], CAP).astype(jnp.bfloat16)
    outgoing_slots = (
        jnp.full((band_total, pair_slots), CAP, jnp.bfloat16)
        .at[destinations, pair_index]
        .set(sent_slot)
    )
    head_bias = position_bias(bias_table)
    own_attended = attend(packed, packed_codes, head_bias, gain_attn, qkv_weight, proj_weight)
    flat_done = feed(own_attended, gain_mlp, hidden_weight, output_weight)
    outgoing = (
        jnp.zeros((band_total, pair_slots, tile_tokens, channels), jnp.bfloat16)
        .at[destinations, pair_index]
        .set(own_attended.reshape(tile_total, tile_tokens, channels))
    )
    incoming, incoming_slots = (
        lax.all_to_all(outgoing, "band", split_axis=0, concat_axis=0, tiled=True),
        lax.all_to_all(outgoing_slots, "band", split_axis=0, concat_axis=0, tiled=True),
    )
    arrived_slot = incoming_slots.reshape(-1).astype(jnp.int32)
    attended = (
        jnp.zeros((CAP, tile_tokens, channels), jnp.bfloat16)
        .at[arrived_slot]
        .set(incoming.reshape(-1, tile_tokens, channels), mode="drop")
    )
    gathered = flat_done[jnp.clip(packed_order, 0, window_total - 1)]
    result = jnp.where(active[:, None, None], gathered, windows)
    band_shifted = (
        result.reshape(win_rows, win_cols, WIN, WIN, channels)
        .transpose(0, 2, 1, 3, 4)
        .reshape(row_count, col_count, channels)
    )
    band_shifted = jnp.roll(band_shifted, SHIFT, axis=1)
    upper_rows = from_behind(band_shifted[row_count - SHIFT :], "band", 1)
    restored = jnp.concatenate([upper_rows, band_shifted[: row_count - SHIFT]], axis=0)
    return (restored, attended)


def solution(mesh):
    in_specs = (
        P(("img", "band"), None, None),
        P(("img", "band"), None),
        P(("img", "band")),
        P(("img", "band"), None),
        P(("img", "band"), None),
        P(),
        P(),
        P(),
        P(),
        P(),
        P(),
        P(),
    )
    out_specs = (P(("img", "band"), None, None), P(("img", "band"), None, None))
    return jax.shard_map(shards, mesh=mesh, in_specs=in_specs, out_specs=out_specs, check_vma=False)
```

profile of v0, /device:TPU:8, one launch (start us, length us, event | category | flops | bytes accessed | tf_op | source)
XLA Modules:
  0.0 171.9 jit_solution(14152191948323769649)
XLA Ops:
  0.7 1.7 fusion.72
  2.7 9.9 %collective-permute-start = (bf16[4,256,180]{2,1,0:T(8,128)(2,1)S(1)}, bf16[4,256,180]{2,1,0:T(8,128)(2,1)S(1)}, u32[]{:S(2)}, u32[]{:S(2)}) collective-permute-start(bf16[4,256,180]{2,1,0:T(8,128)(2,1)S(1)} %copy.93), channel_id=1, source_target_pairs={{0,252},{4,0},{8,4},{12,8},{16,12},{20,16},{24,20},{28,24},{32,28}... | collective-permute-start | bytes 1105928 | tf_op jit(solution)/shard_map/ppermute | solution.py:20
  14.7 5.4 %all-to-all-start = ((bf16[64,1,1]{2,1,0:T(2,128)(2,1)}), bf16[64,1,1]{2,1,0:T(2,128)(2,1)}, u32[]{:S(2)}, u32[]{:S(2)}) async-start(bf16[64,1,1]{2,1,0:T(2,128)(2,1)} %copy.85), calls=%async_computation | async-start | bytes 65536 | tf_op jit(solution)/shard_map/all_to_all | solution.py:161
  20.7 0.8 reshape.421
  22.7 2.6 %fusion.2 = f32[4096,6]{0,1:T(8,128)S(1)} fusion(f32[225,6]{0,1:T(8,128)S(1)} %copy-done.13, s32[4096]{0:T(1024)S(1)} %add.237), kind=kOutput, calls=%fused_computation.13 | convolution fusion | flops 67276800 | bytes 120088 | tf_op jit(solution)/shard_map/dot_general | solution.py:41
  25.5 1.3 compare_select_fusion
  27.1 1.4 copy_bitcast_fusion
  28.6 3.8 %scatter_fusion = bf16[33,64,180]{2,1,0:T(8,128)(2,1)S(1)} fusion(bf16[33,64,180]{2,1,0:T(8,128)(2,1)S(1)} %broadcast_in_dim.32, s32[32]{0:T(128)S(1)} %get-tuple-element.13, bf16[32,64,180]{2,1,0:T(8,128)(2,1)} %copy_bitcast_fusion), kind=kCustom, calls=%fused_computation.1 | custom fusion | bytes 2211968 | tf_op jit(solution)/shard_map/scatter | solution.py:134
  33.8 1.5 fusion.33
  35.3 10.5 %fusion.3 = f32[32,6,64,64]{2,3,1,0:T(8,128)S(1)} fusion(f32[32,64,3,6,30]{1,4,3,2,0:T(8,128)S(1)} %fusion.33), kind=kOutput, calls=%fused_computation.15 | convolution fusion | flops 283484160 | bytes 9437184 | tf_op jit(solution)/shard_map/wqhd,wkhd->whqk/dot_general | solution.py:67
  45.8 3.7 %fusion.73 = (f32[32,6,64]{2,1,0:T(8,128)S(1)}, f32[32,6,64,64]{2,3,1,0:T(8,128)}) fusion(f32[32,6,64,64]{2,3,1,0:T(8,128)S(1)} %fusion.3, f32[32,64,64]{1,2,0:T(8,128)S(1)} %copy-done.7, f32[6,64,64]{1,2,0:T(8,128)S(1)} %bitcast.92), kind=kOutput, calls=%fused_computation.124 | output fusion | flops 4718655 | bytes 6963200 | tf_op jit(solution)/shard_map/sub | solution.py:70
  49.5 3.8 %fusion.29 = bf16[32,64,6,30]{1,3,2,0:T(8,128)(2,1)S(1)} fusion(f32[32,6,64,64]{2,3,1,0:T(8,128)} %get-tuple-element.17, f32[32,6,64]{2,1,0:T(8,128)S(1)} %get-tuple-element.16, f32[32,64,3,6,30]{1,4,3,2,0:T(8,128)S(1)} %fusion.33), kind=kOutput, calls=%fused_computation.48 | convolution fusion | flops 49127424 | bytes 5586944 | tf_op jit(solution)/shard_map/whqk,wkhd->wqhd/dot_general | solution.py:71
  53.4 2.1 %copy.81 = bf16[32,64,6,30]{1,0,3,2:T(8,128)(2,1)} copy(bf16[32,64,6,30]{1,3,2,0:T(8,128)(2,1)S(1)} %fusion.29) | data formatting | bytes 1474560 | tf_op jit(solution)/shard_map/convert_element_type | solution.py:72
  55.5 2.6 %convert_element_type.113 = bf16[2048,180]{0,1:T(8,128)(2,1)S(1)} reshape(bf16[32,64,6,30]{1,0,3,2:T(8,128)(2,1)} %copy.81) | data formatting | bytes 1474560 | tf_op jit(solution)/shard_map/convert_element_type | solution.py:72
  58.1 1.7 copy.82
  59.8 1.8 %convert_reduce_fusion = (f32[2048]{0:T(1024)S(1)}, bf16[2048,180]{0,1:T(8,128)(2,1)S(1)}) fusion(f32[2048,180]{0,1:T(8,128)} %copy.82, bf16[2048,180]{0,1:T(8,128)(2,1)S(1)} %convert_element_type.113, bf16[180,180]{1,0:T(8,128)(2,1)S(1)} %copy-done.9), kind=kOutput, calls=%fused_computation.35 | convolution fusion | flops 134182912 | bytes 3022112 | tf_op jit(solution)/shard_map/dot_general | solution.py:73
  62.5 1.1 copy.86
  63.9 2.2 %scatter_fusion.1 = bf16[64,128,180]{1,2,0:T(8,128)(2,1)S(1)} fusion(bf16[64,128,180]{1,2,0:T(8,128)(2,1)S(1)} %broadcast.482, s32[16]{0:T(128)S(1)} %fusion.63, bf16[16,128,180]{1,2,0:T(8,128)(2,1)} %copy.86), kind=kCustom, calls=%fused_computation.4 | custom fusion | bytes 2211904 | tf_op jit(solution)/shard_map/scatter | solution.py:157
  66.1 1.6 copy-done.1
  67.7 12.8 %all-to-all-start.1 = ((bf16[64,1,128,180]{2,3,1,0:T(8,128)(2,1)}), bf16[64,1,128,180]{2,3,1,0:T(8,128)(2,1)S(1)}, u32[]{:S(2)}, u32[]{:S(2)}) async-start(bf16[64,1,128,180]{2,3,1,0:T(8,128)(2,1)} %bitcast.84), calls=%async_computation.1 | async-start | bytes 6029312 | tf_op jit(solution)/shard_map/all_to_all | solution.py:160
  80.7 1.3 fusion.26
  82.1 3.7 %fusion.18 = bf16[2048,180]{0,1:T(8,128)(2,1)} fusion(bf16[360,180]{0,1:T(8,128)(2,1)S(1)} %copy-done, bf16[2048,180]{0,1:T(8,128)(2,1)} %copy-done.4, bf16[180,360]{1,0:T(8,128)(2,1)S(1)} %copy-done.12, f32[180]{0:T(256)S(1)} %copy-done.14, f32[2048]{0:T(1024)S(1)} %add_rsqrt_fusion.1, f32[2048]{0:T(1024)S(1)} %broadcast_multiply_fusion.1), kind=kOutput, calls=%fused_computation.33 | convolution fusion | flops 540426240 | bytes 1750864 | tf_op jit(solution)/shard_map/dot_general | solution.py:84
  85.8 2.2 %copy.83 = bf16[2048,180]{1,0:T(8,128)(2,1)} copy(bf16[2048,180]{0,1:T(8,128)(2,1)} %fusion.18) | data formatting | bytes 1474560 | tf_op jit(solution)/shard_map/convert_element_type | solution.py:87
  88.0 2.8 %gather_fusion = bf16[32,64,180]{2,1,0:T(8,128)(2,1)} fusion(bf16[32,64,180]{2,1,0:T(8,128)(2,1)} %bitcast.89, s32[1024]{0:T(1024)S(1)} %pad_clamp_fusion), kind=kCustom, calls=%fused_computation | custom fusion | bytes 1474688 | tf_op jit(solution)/shard_map/gather | solution.py:169
  90.8 1.9 %fusion.38 = bf16[8,256,180]{2,1,0:T(8,128)(2,1)S(1)} fusion(pred[32]{0:T(512)(128)(4,1)S(1)} %bitcast_and_fusion, bf16[4,256,180]{2,1,0:T(8,128)(2,1)} %copy-done.5, bf16[4,256,180]{2,1,0:T(8,128)(2,1)} %copy-done.3, bf16[8,252,180]{2,1,0:T(8,128)(2,1)} %copy-done.2, bf16[32,64,180]{2,1,0:T(8,128)(2,1)} %gather_fusion), kind=kLoop, calls=%fused_computation.60 | loop fusion | flops 2580480 | bytes 2937632 | tf_op jit(solution)/shard_map/reshape | solution.py:174
  92.9 3.2 %collective-permute-start.1 = (bf16[4,256,180]{2,1,0:T(8,128)(2,1)S(1)}, bf16[4,256,180]{2,1,0:T(8,128)(2,1)S(1)}, u32[]{:S(2)}, u32[]{:S(2)}) collective-permute-start(bf16[4,256,180]{2,1,0:T(8,128)(2,1)S(1)} %fusion.51), channel_id=1, source_target_pairs={{0,4},{4,8},{8,12},{12,16},{16,20},{20,24},{24,28},{28,32},{32,36}... | collective-permute-start | bytes 1105928 | tf_op jit(solution)/shard_map/ppermute | solution.py:20
  96.1 2.0 %convert_reduce_fusion.2 = s32[64]{0:T(128)S(1)} fusion(bf16[64,1,1]{2,1,0:T(2,128)(2,1)} %all-to-all-done), kind=kLoop, calls=%fused_computation.75 | loop fusion | flops 64 | bytes 384 | tf_op jit(solution)/shard_map/convert_element_type | solution.py:163
  98.1 65.3 %collective-permute-done.1 = bf16[4,256,180]{2,1,0:T(8,128)(2,1)S(1)} collective-permute-done((bf16[4,256,180]{2,1,0:T(8,128)(2,1)S(1)}, bf16[4,256,180]{2,1,0:T(8,128)(2,1)S(1)}, u32[]{:S(2)}, u32[]{:S(2)}) %collective-permute-start.1) | collective-permute-done | bytes 368672 | tf_op jit(solution)/shard_map/ppermute | solution.py:20
  163.4 1.2 fusion.35
  164.6 2.3 %copy.88 = bf16[8,256,180]{1,0,2:T(8,128)(2,1)} copy(bf16[8,256,180]{2,1,0:T(8,128)(2,1)} %fusion.35) | data formatting | bytes 1474560
  166.9 4.1 %scatter_fusion.2 = bf16[8,128,180]{1,2,0:T(8,128)(2,1)S(1)} fusion(bf16[8,128,180]{1,2,0:T(8,128)(2,1)S(1)} %broadcast_in_dim.37, s32[64]{0:T(128)S(1)} %fusion.64, bf16[64,128,180]{1,2,0:T(8,128)(2,1)S(1)} %bitcast.83), kind=kCustom, calls=%fused_computation.5 | custom fusion | bytes 8847616 | tf_op jit(solution)/shard_map/scatter | solution.py:167
  171.1 0.8 copy.89
  (76 shorter events, 7.0 us)
Async XLA Ops:
  0.6 81.4 %copy-start = (bf16[360,180]{0,1:T(8,128)(2,1)S(1)}, bf16[360,180]{0,1:T(8,128)(2,1)}, u32[]{:S(2)}) copy-start(bf16[360,180]{0,1:T(8,128)(2,1)} %param.23) | copy-start | bytes 388804
  0.6 12.6 %copy-start.15 = (s32[1,16]{1,0:T(1,128)S(1)}, s32[1,16]{1,0:T(1,128)}, u32[]{:S(2)}) copy-start(s32[1,16]{1,0:T(1,128)} %param.15) | copy-start | bytes 196
  0.7 12.6 %copy-start.16 = (s32[1,16]{1,0:T(1,128)S(1)}, s32[1,16]{1,0:T(1,128)}, u32[]{:S(2)}) copy-start(s32[1,16]{1,0:T(1,128)} %param.16) | copy-start | bytes 196
  0.7 19.7 %copy-start.11 = (s32[1,32]{1,0:T(1,128)S(1)}, s32[1,32]{1,0:T(1,128)}, u32[]{:S(2)}) copy-start(s32[1,32]{1,0:T(1,128)} %param.13) | copy-start | bytes 388
  0.7 19.8 %copy-start.8 = (bf16[180,540]{1,0:T(8,128)(2,1)S(1)}, bf16[180,540]{1,0:T(8,128)(2,1)}, u32[]{:S(2)}) copy-start(bf16[180,540]{1,0:T(8,128)(2,1)} %param.19) | copy-start | bytes 583204
  0.7 22.0 %copy-start.13 = (f32[225,6]{0,1:T(8,128)S(1)}, f32[225,6]{0,1:T(8,128)}, u32[]{:S(2)}) copy-start(f32[225,6]{0,1:T(8,128)} %param.17) | copy-start | bytes 16204
  2.7 24.1 %collective-permute-start = (bf16[4,256,180]{2,1,0:T(8,128)(2,1)S(1)}, bf16[4,256,180]{2,1,0:T(8,128)(2,1)S(1)}, u32[]{:S(2)}, u32[]{:S(2)}) collective-permute-start(bf16[4,256,180]{2,1,0:T(8,128)(2,1)S(1)} %copy.93), channel_id=1, source_target_pairs={{0,252},{4,0},{8,4},{12,8},{16,12},{20,16},{24,20},{28,24},{32,28}... | collective-permute-start | bytes 1105928 | tf_op jit(solution)/shard_map/ppermute | solution.py:20
  14.7 51.4 %all-to-all-start = ((bf16[64,1,1]{2,1,0:T(2,128)(2,1)}), bf16[64,1,1]{2,1,0:T(2,128)(2,1)}, u32[]{:S(2)}, u32[]{:S(2)}) async-start(bf16[64,1,1]{2,1,0:T(2,128)(2,1)} %copy.85), calls=%async_computation | async-start | bytes 65536 | tf_op jit(solution)/shard_map/all_to_all | solution.py:161
  20.4 6.7 %copy-start.3 = (bf16[4,256,180]{2,1,0:T(8,128)(2,1)}, bf16[4,256,180]{2,1,0:T(8,128)(2,1)S(1)}, u32[]{:S(2)}) copy-start(bf16[4,256,180]{2,1,0:T(8,128)(2,1)S(1)} %copy.92) | copy-start | bytes 1105924
  26.8 1.7 copy-start.5
  27.1 1.4 copy-start.2
  32.8 1.0 copy-start.6
  32.8 1.0 copy-start.10
  35.3 10.5 %copy-start.7 = (f32[32,64,64]{1,2,0:T(8,128)S(1)}, f32[32,64,64]{1,2,0:T(8,128)}, u32[]{:S(2)}) copy-start(f32[32,64,64]{1,2,0:T(8,128)} %compare_select_fusion) | copy-start | bytes 1572868
  58.1 1.7 copy-start.9
  61.6 0.9 copy-start.4
  66.1 1.6 copy-start.1
  67.7 14.3 %copy-start.12 = (bf16[180,360]{1,0:T(8,128)(2,1)S(1)}, bf16[180,360]{1,0:T(8,128)(2,1)}, u32[]{:S(2)}) copy-start(bf16[180,360]{1,0:T(8,128)(2,1)} %param.22) | copy-start | bytes 388804
  67.7 14.3 %copy-start.14 = (f32[180]{0:T(256)S(1)}, f32[180]{0:T(256)}, u32[]{:S(2)}) copy-start(f32[180]{0:T(256)} %param.21) | copy-start | bytes 2164
  67.7 99.2 %all-to-all-start.1 = ((bf16[64,1,128,180]{2,3,1,0:T(8,128)(2,1)}), bf16[64,1,128,180]{2,3,1,0:T(8,128)(2,1)S(1)}, u32[]{:S(2)}, u32[]{:S(2)}) async-start(bf16[64,1,128,180]{2,3,1,0:T(8,128)(2,1)} %bitcast.84), calls=%async_computation.1 | async-start | bytes 6029312 | tf_op jit(solution)/shard_map/all_to_all | solution.py:160
  92.9 70.4 %collective-permute-start.1 = (bf16[4,256,180]{2,1,0:T(8,128)(2,1)S(1)}, bf16[4,256,180]{2,1,0:T(8,128)(2,1)S(1)}, u32[]{:S(2)}, u32[]{:S(2)}) collective-permute-start(bf16[4,256,180]{2,1,0:T(8,128)(2,1)S(1)} %fusion.51), channel_id=1, source_target_pairs={{0,4},{4,8},{8,12},{12,16},{16,20},{20,24},{24,28},{28,32},{32,36}... | collective-permute-start | bytes 1105928 | tf_op jit(solution)/shard_map/ppermute | solution.py:20
where the time goes:
time: 174 us; the launch traced here: 172 us
  waiting for transfers between devices  65.3 us (38%)
  local copies, waits for them, and re-layouts  34.5 us (20%)
  starting transfers between devices  31.2 us (18%)
  matrix products  23.9 us (14%)
  other arithmetic  15.1 us (9%)
  between operations  1.78 us (1%)
    ppermute x2, waiting for transfers between devices, from_behind(): return lax.ppermute(value, axis, pairs)  65.3 us
    ppermute x2, starting transfers between devices, from_behind(): return lax.ppermute(value, axis, pairs)  13 us
    all_to_all x1, starting transfers between devices, shards(): lax.all_to_all(outgoing, 'band', split_axis=0, concat_axis=0, tiled=True)  12.8 us
    dot_general x1, matrix products, attend(): jnp.einsum('wqhd,wkhd->whqk', queries, key_part, precision=lax.Precision....  10.5 us
    unnamed x39, local copies, waits for them, and re-layouts  6.07 us
    all_to_all x1, starting transfers between devices, shards(): lax.all_to_all(outgoing_slots, 'band', split_axis=0, concat_axis=0, tiled...  5.38 us
    convert_element_type x2, local copies, waits for them, and re-layouts, attend(): mixed = mixed.reshape(-1, CHAN).astype(jnp.bfloat16)  4.7 us
    scatter x1, local copies, waits for them, and re-layouts, shards(): attended = jnp.zeros((CAP, tile_tokens, channels), jnp.bfloat16).at[arriv...  4.13 us
  transfers between devices with their start and end apart: 4, of which 1 were waited for; matrix products, arithmetic and copies ran while one was open for 37% of the time, Pallas kernels for 0%

commit v1 on v0

v1 whole, which is shorter than its diff:
```python
import functools

import jax
import jax.numpy as jnp
from jax import lax
from jax.experimental import pallas as pl
from jax.experimental.pallas import tpu as pltpu
from jax.sharding import PartitionSpec as P

CHAN = 180
HEADS = 6
HEAD_DIM = CHAN // HEADS
HEAD_PAD = 32
WIN = 8
TOKENS = WIN * WIN
TILE = 2
LANES = TILE * TOKENS
SHIFT = 4
CAP = 8
EPSILON = 1e-05
VMEM_LIMIT = 60 << 20


def from_behind(value, axis, steps):
    count = lax.axis_size(axis)
    pairs = [(source, (source + steps) % count) for source in range(count)]
    return lax.ppermute(value, axis, pairs)


def position_bias(bias_table):
    coords = jnp.arange(TOKENS, dtype=jnp.int32)
    row_pos = coords // WIN
    col_pos = coords % WIN
    table_index = (row_pos[None, :] - row_pos[:, None] + WIN - 1) * (2 * WIN - 1) + (
        col_pos[None, :] - col_pos[:, None] + WIN - 1
    )
    entries = bias_table.shape[0]
    onehot = (table_index.reshape(1, -1) == jnp.arange(entries, dtype=jnp.int32)[:, None]).astype(
        jnp.float32
    )
    looked = lax.dot_general(
        bias_table, onehot, (((0,), (0,)), ((), ())), precision=lax.Precision.HIGHEST
    )
    looked = looked.reshape(-1, TOKENS, TOKENS)
    return jnp.concatenate([looked, looked], axis=2)


def norm_columns(values, gain):
    center = values - jnp.sum(values, axis=0, keepdims=True) * (1.0 / CHAN)
    spread = jnp.sum(center * center, axis=0, keepdims=True) * (1.0 / CHAN)
    return (center * lax.rsqrt(spread + EPSILON) * gain).astype(jnp.bfloat16)


def split_two(values):
    high = values.astype(jnp.bfloat16)
    low = (values - high.astype(jnp.float32)).astype(jnp.bfloat16)
    return high, low


def attend_tile(x_cols, mask, gain, qkv_t, proj_t, bias_ref):
    lane = lax.broadcasted_iota(jnp.int32, (TOKENS, LANES), 1)
    first = lane < TOKENS
    normed = norm_columns(x_cols, gain)
    qkv = jnp.dot(qkv_t, normed, preferred_element_type=jnp.float32)
    mixed = []
    width = HEADS * HEAD_PAD
    for head in range(HEADS):
        at = head * HEAD_PAD
        query = qkv[at : at + HEAD_PAD] * HEAD_DIM ** (-0.5)
        key = qkv[width + at : width + at + HEAD_PAD]
        value = qkv[2 * width + at : 2 * width + at + HEAD_PAD].astype(jnp.bfloat16)
        query_high, query_low = split_two(query)
        key_high, key_low = split_two(key)
        left = jnp.concatenate([key_high, key_low, key_high], axis=0)
        right = jnp.concatenate([query_high, query_high, query_low], axis=0)
        full = lax.dot_general(
            left, right, (((0,), (0,)), ((), ())), preferred_element_type=jnp.float32
        )
        scores = jnp.where(first, full[:TOKENS], full[TOKENS:])
        scores = (scores + bias_ref[head]) + mask
        top = jnp.max(scores, axis=0, keepdims=True)
        grown = jnp.exp(scores - top)
        total = jnp.sum(grown, axis=0, keepdims=True)
        weights = grown * (1.0 / total)
        spread = jnp.concatenate(
            [jnp.where(first, weights, 0.0), jnp.where(first, 0.0, weights)], axis=0
        ).astype(jnp.bfloat16)
        mixed.append(jnp.dot(value, spread, preferred_element_type=jnp.float32).astype(jnp.bfloat16))
    mixed = jnp.concatenate(mixed, axis=0)
    projected = jnp.dot(proj_t, mixed, preferred_element_type=jnp.float32)
    return (x_cols + projected).astype(jnp.bfloat16)


def feed_tile(state, gain, hidden_t, output_t):
    state = state.astype(jnp.float32)
    normed = norm_columns(state, gain)
    hidden = jnp.dot(hidden_t, normed, preferred_element_type=jnp.float32)
    inner = jax.nn.gelu(hidden).astype(jnp.bfloat16)
    return state + jnp.dot(output_t, inner, preferred_element_type=jnp.float32)


def load_windows(pixels_ref, halo_ref, windows):
    count = windows.shape[0]

    def one(ref, source, row):
        values = ref[source].astype(jnp.float32)
        values = jnp.concatenate([values[SHIFT:], values[:SHIFT]], axis=0)
        windows[:, pl.ds(pl.multiple_of(row * WIN, WIN), WIN), :] = values.reshape(count, WIN, CHAN)

    for row in range(WIN - SHIFT):
        one(pixels_ref, row + SHIFT, row)
    for row in range(SHIFT):
        one(halo_ref, row, row + WIN - SHIFT)


def order_windows(keep_ref, count_ref, order):
    total = order.shape[0] - 1
    for place in range(total + 1):
        order[place] = total

    def step(index, position):
        kept = keep_ref[index]
        live = jnp.logical_and(kept == 1, position < count_ref[0])
        order[jnp.where(live, position, total)] = index
        return position + kept

    lax.fori_loop(0, total, step, jnp.int32(0))
    order[total] = total


def region_mask(last_band, last_first, last_second):
    key = lax.broadcasted_iota(jnp.int32, (TOKENS, LANES), 0)
    lane = lax.broadcasted_iota(jnp.int32, (TOKENS, LANES), 1)
    query = lane & (TOKENS - 1)
    rows_differ = ((key ^ query) & (SHIFT * WIN)) != 0
    cols_differ = ((key ^ query) & SHIFT) != 0
    last_col = jnp.where(lane < TOKENS, last_first, last_second)
    row_part = jnp.where(rows_differ, last_band, 0)
    col_part = jnp.where(cols_differ, last_col, 0)
    return jnp.where((row_part | col_part) != 0, -100.0, 0.0)


def attend_kernel(
    keep_ref, count_ref, band_ref, pixels_ref, halo_ref, gain_ref, qkv_ref, proj_ref, bias_ref, out_ref, windows, order
):
    total = windows.shape[0] - 1
    load_windows(pixels_ref, halo_ref, windows.at[pl.ds(0, total)])
    windows[total] = jnp.zeros((TOKENS, CHAN), jnp.float32)
    order_windows(keep_ref, count_ref, order)

    def step(tile, carry):
        one = order[tile * TILE]
        two = order[tile * TILE + 1]
        x_cols = jnp.concatenate([windows[one], windows[two]], axis=0).T
        mask = region_mask(
            band_ref[0], (one == total - 1).astype(jnp.int32), (two == total - 1).astype(jnp.int32)
        )
        out_ref[tile] = attend_tile(x_cols, mask, gain_ref[...], qkv_ref[...], proj_ref[...], bias_ref)
        return carry

    lax.fori_loop(0, out_ref.shape[0], step, 0, unroll=2)


def feed_kernel(
    keep_ref, count_ref, pixels_ref, halo_ref, state_ref, gain_ref, hidden_ref, output_ref, own_ref, sent_ref, windows, order
):
    total = windows.shape[0] - 1
    load_windows(pixels_ref, halo_ref, windows.at[pl.ds(0, total)])
    order_windows(keep_ref, count_ref, order)

    def step(tile, carry):
        done = feed_tile(state_ref[tile], gain_ref[...], hidden_ref[...], output_ref[...]).T
        windows[order[tile * TILE]] = done[:TOKENS]
        windows[order[tile * TILE + 1]] = done[TOKENS:]
        return carry

    lax.fori_loop(0, state_ref.shape[0], step, 0, unroll=2)
    for row in range(WIN):
        values = windows[0:total, row * WIN : (row + 1) * WIN, :].reshape(total * WIN, CHAN)
        values = jnp.concatenate([values[-SHIFT:], values[:-SHIFT]], axis=0).astype(jnp.bfloat16)
        if row < WIN - SHIFT:
            own_ref[row] = values
        else:
            sent_ref[row - WIN + SHIFT] = values


def pad_heads(weight):
    groups = weight.reshape(weight.shape[0], -1, HEAD_DIM)
    groups = jnp.pad(groups, ((0, 0), (0, 0), (0, HEAD_PAD - HEAD_DIM)))
    return groups.reshape(weight.shape[0], -1)


SMEM = pl.BlockSpec(memory_space=pltpu.SMEM)
VMEM = pl.BlockSpec(memory_space=pltpu.VMEM)


def shards(
    pixels,
    keep_mask,
    band_counts,
    plan_dest,
    plan_slot,
    bias_table,
    gain_attn,
    qkv_weight,
    proj_weight,
    gain_mlp,
    hidden_weight,
    output_weight,
):
    band_total = lax.axis_size("band")
    band_index = lax.axis_index("band")
    row_count, col_count, channels = pixels.shape
    window_total = keep_mask.shape[1]
    tile_total = window_total // TILE
    tile_tokens = TILE * TOKENS
    halo = from_behind(pixels[:SHIFT], "band", -1)
    last_band = (band_index == band_total - 1).astype(jnp.int32).reshape(1)
    keep = keep_mask.reshape(window_total)
    kept_count = band_counts[0]
    attended = pl.pallas_call(
        attend_kernel,
        out_shape=jax.ShapeDtypeStruct((tile_total, CHAN, LANES), jnp.bfloat16),
        in_specs=[SMEM] * 3 + [VMEM] * 6,
        out_specs=VMEM,
        scratch_shapes=[
            pltpu.VMEM((window_total + 1, TOKENS, CHAN), jnp.float32),
            pltpu.SMEM((window_total + 1,), jnp.int32),
        ],
        compiler_params=pltpu.CompilerParams(vmem_limit_bytes=VMEM_LIMIT),
        cost_estimate=pl.CostEstimate(flops=2 * 10**9, bytes_accessed=2 * 10**6, transcendentals=10**6),
        name="attend",
    )(
        keep,
        band_counts,
        last_band,
        pixels,
        halo,
        gain_attn.reshape(CHAN, 1),
        pad_heads(qkv_weight).T,
        pad_heads(proj_weight.T),
        position_bias(bias_table),
    )
    tile_ids = jnp.arange(tile_total, dtype=jnp.int32)
    tile_live = tile_ids * TILE < kept_count
    destinations = plan_dest[0]
    sent_slot = jnp.where(tile_live, plan_slot[0], CAP).astype(jnp.bfloat16)
    outgoing_slots = jnp.full((band_total, 1), CAP, jnp.bfloat16).at[destinations, 0].set(sent_slot)
    outgoing = jnp.zeros((band_total, CHAN, LANES), jnp.bfloat16).at[destinations].set(attended)
    incoming = lax.all_to_all(outgoing, "band", split_axis=0, concat_axis=0, tiled=True)
    incoming_slots = lax.all_to_all(outgoing_slots, "band", split_axis=0, concat_axis=0, tiled=True)
    own, sent = pl.pallas_call(
        feed_kernel,
        out_shape=[
            jax.ShapeDtypeStruct((row_count - SHIFT, col_count, CHAN), jnp.bfloat16),
            jax.ShapeDtypeStruct((SHIFT, col_count, CHAN), jnp.bfloat16),
        ],
        in_specs=[SMEM] * 2 + [VMEM] * 6,
        out_specs=[VMEM, VMEM],
        scratch_shapes=[
            pltpu.VMEM((window_total + 1, TOKENS, CHAN), jnp.float32),
            pltpu.SMEM((window_total + 1,), jnp.int32),
        ],
        compiler_params=pltpu.CompilerParams(vmem_limit_bytes=VMEM_LIMIT),
        cost_estimate=pl.CostEstimate(flops=2 * 10**9, bytes_accessed=2 * 10**6, transcendentals=10**6),
        name="feed",
    )(
        keep,
        band_counts,
        pixels,
        halo,
        attended,
        gain_mlp.reshape(CHAN, 1),
        hidden_weight.T,
        output_weight.T,
    )
    arrived_slot = incoming_slots.reshape(-1).astype(jnp.int32)
    work = (
        jnp.zeros((CAP, CHAN, LANES), jnp.bfloat16).at[arrived_slot].set(incoming, mode="drop")
    )
    work = jnp.transpose(work, (0, 2, 1))
    upper_rows = from_behind(sent, "band", 1)
    restored = jnp.concatenate([upper_rows, own], axis=0)
    return (restored, work)


def solution(mesh):
    sharded = P(("img", "band"))
    in_specs = (
        P(("img", "band"), None, None),
        P(("img", "band"), None),
        sharded,
        P(("img", "band"), None),
        P(("img", "band"), None),
    ) + (P(),) * 7
    out_specs = (P(("img", "band"), None, None), P(("img", "band"), None, None))
    return jax.shard_map(shards, mesh=mesh, in_specs=in_specs, out_specs=out_specs, check_vma=False)
```

time: 174 us -> 164 us (0.943)
  Pallas kernels: 0 us -> 37 us
  matrix products: 23.9 us -> 1.3 us
  local copies, waits for them, and re-layouts: 34.5 us -> 20.2 us
  other arithmetic: 15.1 us -> 5.62 us
    pallas_call x0 -> x2, Pallas kernels: none -> 37 us  [the longest x1 26.7 us: shards(): pl.pallas_call(attend_kernel, out_shape=jax.ShapeDtypeStruct((tile_total,...]
    dot_general x6 -> x1, matrix products: 23.9 us -> 1.3 us  [position_bias(): lax.dot_general(bias_table, onehot, (((0,), (0,)), ((), ())), precision=l...]
    convert_element_type x5 -> x0, local copies, waits for them, and re-layouts: 8.68 us -> none  [the longest x2 4.7 us: attend(): mixed = mixed.reshape(-1, CHAN).astype(jnp.bfloat16)]
    scatter x5 -> x3, local copies, waits for them, and re-layouts: 11.4 us -> 7.54 us  [the longest x1 4.13 us: shards(): jnp.zeros((CAP, CHAN, LANES), jnp.bfloat16).at[arrived_slot]]
    sub x1 -> x0, other arithmetic: 3.74 us -> none  [attend(): weights = jax.nn.softmax(scores, axis=-1).astype(jnp.bfloat16)]
    reshape x2 -> x0, other arithmetic: 3.28 us -> none  [the longest x1 1.91 us: shards(): band_shifted = result.reshape(win_rows, win_cols, WIN, WIN, channels).tra...]
    gather x1 -> x0, local copies, waits for them, and re-layouts: 2.81 us -> none  [shards(): gathered = flat_done[jnp.clip(packed_order, 0, window_total - 1)]]
    reduce_sum x3 -> x0, other arithmetic: 2.33 us -> none  [the longest x2 1.99 us: layer_norm(): spread = jnp.mean(center * center, axis=-1, keepdims=True)]
  transfers between devices with their start and end apart: 4 -> 4, of which waited for: 1 -> 1; matrix products, arithmetic and copies ran while one was open for 37% -> 12% of each run, Pallas kernels for 0% -> 23%
where the time goes in v1:
time: 164 us; the launch traced here: 163 us
  waiting for transfers between devices  66.4 us (40%)
  Pallas kernels  37 us (23%)
  starting transfers between devices  31 us (19%)
  local copies, waits for them, and re-layouts  20.2 us (12%)
  other arithmetic  5.62 us (3%)
    ppermute x2, waiting for transfers between devices, from_behind(): return lax.ppermute(value, axis, pairs)  66.4 us
    pallas_call x1, Pallas kernels, shards(): pl.pallas_call(attend_kernel, out_shape=jax.ShapeDtypeStruct((tile_total,...  26.7 us
    ppermute x2, starting transfers between devices, from_behind(): return lax.ppermute(value, axis, pairs)  12.9 us
    all_to_all x1, starting transfers between devices, shards(): lax.all_to_all(outgoing, 'band', split_axis=0, concat_axis=0, tiled=True)  12.9 us
    pallas_call x1, Pallas kernels, shards(): pl.pallas_call(feed_kernel, out_shape=[jax.ShapeDtypeStruct((row_count -...  10.3 us
    unnamed x23, local copies, waits for them, and re-layouts  6.48 us
    all_to_all x1, starting transfers between devices, shards(): lax.all_to_all(outgoing_slots, 'band', split_axis=0, concat_axis=0, tiled...  5.12 us
    scatter x1, local copies, waits for them, and re-layouts, shards(): jnp.zeros((CAP, CHAN, LANES), jnp.bfloat16).at[arrived_slot]  4.13 us
  transfers between devices with their start and end apart: 4, of which 1 were waited for; matrix products, arithmetic and copies ran while one was open for 12% of the time, Pallas kernels for 23%

profile of v1, /device:TPU:8, one launch (start us, length us, event | category | flops | bytes accessed | tf_op | source)
XLA Modules:
  0.0 162.9 jit_solution(11846942858226932986)
XLA Ops:
  0.7 1.6 copy.48.pixels_ref
  2.3 9.9 %collective-permute-start = (bf16[4,256,180]{2,1,0:T(8,128)(2,1)S(1)}, bf16[4,256,180]{2,1,0:T(8,128)(2,1)S(1)}, u32[]{:S(2)}, u32[]{:S(2)}) collective-permute-start(bf16[4,256,180]{2,1,0:T(8,128)(2,1)S(1)} %slice.6), channel_id=1, source_target_pairs={{0,252},{4,0},{8,4},{12,8},{16,12},{20,16},{24,20},{28,24},{32,28}... | collective-permute-start | bytes 1105928 | tf_op jit(solution)/shard_map/ppermute | solution.py:27
  12.8 0.7 fusion.2
  13.5 0.7 fusion.1
  14.2 0.7 scatter_custom_fusion
  14.8 0.7 copy.50
  15.6 5.1 %all-to-all-start = ((bf16[64,1,1]{2,1,0:T(2,128)(2,1)}), bf16[64,1,1]{2,1,0:T(2,128)(2,1)S(1)}, u32[]{:S(2)}, u32[]{:S(2)}) async-start(bf16[64,1,1]{2,1,0:T(2,128)(2,1)} %copy.50), calls=%async_computation | async-start | bytes 65536 | tf_op jit(solution)/shard_map/all_to_all | solution.py:251
  20.7 0.1 add_add_fusion
  20.8 0.1 add.83
  20.9 1.3 convolution_bitcast_fusion
  22.2 0.1 reshape.176
  22.3 0.2 copy.43
  22.4 0.1 reshape.172
  22.6 0.8 pad.9
  23.4 0.7 copy.46.proj_ref
  24.1 0.8 copy.45.gain_ref
  24.9 0.8 pad_maximum_fusion.1.bias_ref
  25.7 0.8 copy-done.8
  26.5 26.7 %attend.1.state_ref = bf16[16,180,128]{2,1,0:T(8,128)(2,1)} custom-call(s32[32]{0:T(128)} %bitcast.41, s32[1]{0:T(128)} %copy.55.count_ref, s32[1]{0:T(128)} %bitcast.1.band_ref, bf16[8,256,180]{2,1,0:T(8,128)(2,1)} %copy-done.1, bf16[4,256,180]{2,1,0:T(8,128)(2,1)} %copy-done.8, f32[180,1]{1,0:T(8,128)} %copy.45.gain_ref, bf16[576,180]{1,0:T(8,128)(2,1)} %bitcast.34, ...), custom_call_target="tpu_custom_call" | custom-call | flops 2000000000 | bytes 2000000 | tf_op jit(solution)/shard_map/attend/pallas_call | solution.py:221
  53.1 2.0 %broadcast_in_dim.24 = bf16[64,180,128]{2,1,0:T(8,128)(2,1)} broadcast(bf16[]{:T(256)} %constant.56.clone.1), dimensions={} | broadcast | bytes 2949122 | tf_op jit(solution)/shard_map/broadcast_in_dim | solution.py:249
  55.2 2.7 %scatter_fusion = bf16[64,180,128]{2,1,0:T(8,128)(2,1)} fusion(bf16[64,180,128]{2,1,0:T(8,128)(2,1)} %broadcast_in_dim.24, s32[16]{0:T(128)S(1)} %fusion.2, bf16[16,180,128]{2,1,0:T(8,128)(2,1)S(1)} %copy-done.2), kind=kCustom, calls=%fused_computation.1 | custom fusion | bytes 2211904 | tf_op jit(solution)/shard_map/scatter | solution.py:249
  57.9 12.9 %all-to-all-start.1 = ((bf16[64,180,128]{2,1,0:T(8,128)(2,1)}), bf16[64,180,128]{2,1,0:T(8,128)(2,1)S(1)}, u32[]{:S(2)}, u32[]{:S(2)}) async-start(bf16[64,180,128]{2,1,0:T(8,128)(2,1)} %scatter_fusion), calls=%async_computation.1 | async-start | bytes 6029312 | tf_op jit(solution)/shard_map/all_to_all | solution.py:250
  70.8 0.8 copy.47
  71.6 0.8 copy.49.gain_ref
  72.4 10.3 %feed.1 = (bf16[4,256,180]{2,1,0:T(8,128)(2,1)}, bf16[4,256,180]{2,1,0:T(8,128)(2,1)}) custom-call(s32[32]{0:T(128)} %bitcast.42, s32[1]{0:T(128)} %copy.55.count_ref, bf16[8,256,180]{2,1,0:T(8,128)(2,1)} %copy-done.1, bf16[4,256,180]{2,1,0:T(8,128)(2,1)} %copy-done.8, bf16[16,180,128]{2,1,0:T(8,128)(2,1)} %attend.1.state_ref, f32[180,1]{1,0:T(8,128)} %copy.49.gain_ref, ...), custom_call_target="tpu_custom_call" | custom-call | flops 2000000000 | bytes 2000000 | tf_op jit(solution)/shard_map/feed/pallas_call | solution.py:252
  82.7 3.1 %collective-permute-start.1 = (bf16[4,256,180]{2,1,0:T(8,128)(2,1)}, bf16[4,256,180]{2,1,0:T(8,128)(2,1)S(1)}, u32[]{:S(2)}, u32[]{:S(2)}) collective-permute-start(bf16[4,256,180]{2,1,0:T(8,128)(2,1)} %get-tuple-element.4), channel_id=1, source_target_pairs={{0,4},{4,8},{8,12},{12,16},{16,20},{20,24},{24,28},{28,32},{32,36}... | collective-permute-start | bytes 1105928 | tf_op jit(solution)/shard_map/ppermute | solution.py:27
  85.8 1.2 convert_reduce_fusion
  87.0 66.4 %collective-permute-done.1 = bf16[4,256,180]{2,1,0:T(8,128)(2,1)S(1)} collective-permute-done((bf16[4,256,180]{2,1,0:T(8,128)(2,1)}, bf16[4,256,180]{2,1,0:T(8,128)(2,1)S(1)}, u32[]{:S(2)}, u32[]{:S(2)}) %collective-permute-start.1) | collective-permute-done | bytes 368672 | tf_op jit(solution)/shard_map/ppermute | solution.py:27
  153.4 2.2 %pad_maximum_fusion = bf16[8,256,180]{2,1,0:T(8,128)(2,1)} fusion(bf16[4,256,180]{2,1,0:T(8,128)(2,1)} %get-tuple-element.5, bf16[4,256,180]{2,1,0:T(8,128)(2,1)S(1)} %collective-permute-done.1), kind=kLoop, calls=%fused_computation.6 | loop fusion | flops 368640 | bytes 1474560 | tf_op jit(solution)/shard_map/concatenate | solution.py:283
  155.6 2.3 %copy.51 = bf16[8,256,180]{1,0,2:T(8,128)(2,1)} copy(bf16[8,256,180]{2,1,0:T(8,128)(2,1)} %pad_maximum_fusion) | data formatting | bytes 1474560
  158.0 4.1 %scatter_fusion.1 = bf16[8,180,128]{2,1,0:T(8,128)(2,1)S(1)} fusion(bf16[8,180,128]{2,1,0:T(8,128)(2,1)S(1)} %broadcast_in_dim.10, s32[64]{0:T(128)S(1)} %fusion.3, bf16[64,180,128]{2,1,0:T(8,128)(2,1)S(1)} %all-to-all-done.1), kind=kCustom, calls=%fused_computation.2 | custom fusion | bytes 8847616 | tf_op jit(solution)/shard_map/scatter | solution.py:279
  162.1 0.8 copy.52
  (26 shorter events, 0.2 us)
Async XLA Ops:
  0.6 20.2 %copy-start = (f32[225,6]{0,1:T(8,128)S(1)}, f32[225,6]{0,1:T(8,128)}, u32[]{:S(2)}) copy-start(f32[225,6]{0,1:T(8,128)} %param.17) | copy-start | bytes 16204
  0.6 21.6 %copy-start.3 = (bf16[180,540]{1,0:T(8,128)(2,1)S(1)}, bf16[180,540]{1,0:T(8,128)(2,1)}, u32[]{:S(2)}) copy-start(bf16[180,540]{1,0:T(8,128)(2,1)} %param.19) | copy-start | bytes 583204
  0.7 21.9 %copy-start.5 = (bf16[180,180]{1,0:T(8,128)(2,1)S(1)}, bf16[180,180]{1,0:T(8,128)(2,1)}, u32[]{:S(2)}) copy-start(bf16[180,180]{1,0:T(8,128)(2,1)} %param.20) | copy-start | bytes 194404
  0.7 23.5 %copy-start.6 = (f32[180]{0:T(256)S(1)}, f32[180]{0:T(256)}, u32[]{:S(2)}) copy-start(f32[180]{0:T(256)} %param.18) | copy-start | bytes 2164
  2.3 23.4 %copy-start.1 = (bf16[8,256,180]{2,1,0:T(8,128)(2,1)}, bf16[8,256,180]{2,1,0:T(8,128)(2,1)S(1)}, u32[]{:S(2)}) copy-start(bf16[8,256,180]{2,1,0:T(8,128)(2,1)S(1)} %copy.48.pixels_ref) | copy-start | bytes 2211844
  2.3 23.4 %collective-permute-start = (bf16[4,256,180]{2,1,0:T(8,128)(2,1)S(1)}, bf16[4,256,180]{2,1,0:T(8,128)(2,1)S(1)}, u32[]{:S(2)}, u32[]{:S(2)}) collective-permute-start(bf16[4,256,180]{2,1,0:T(8,128)(2,1)S(1)} %slice.6), channel_id=1, source_target_pairs={{0,252},{4,0},{8,4},{12,8},{16,12},{20,16},{24,20},{28,24},{32,28}... | collective-permute-start | bytes 1105928 | tf_op jit(solution)/shard_map/ppermute | solution.py:27
  15.6 42.3 %all-to-all-start = ((bf16[64,1,1]{2,1,0:T(2,128)(2,1)}), bf16[64,1,1]{2,1,0:T(2,128)(2,1)S(1)}, u32[]{:S(2)}, u32[]{:S(2)}) async-start(bf16[64,1,1]{2,1,0:T(2,128)(2,1)} %copy.50), calls=%async_computation | async-start | bytes 65536 | tf_op jit(solution)/shard_map/all_to_all | solution.py:251
  25.7 0.8 copy-start.8
  53.1 2.0 %copy-start.2 = (bf16[16,180,128]{2,1,0:T(8,128)(2,1)S(1)}, bf16[16,180,128]{2,1,0:T(8,128)(2,1)}, u32[]{:S(2)}) copy-start(bf16[16,180,128]{2,1,0:T(8,128)(2,1)} %attend.1.state_ref) | copy-start | bytes 2211844
  57.9 12.9 %copy-start.4 = (bf16[180,360]{1,0:T(8,128)(2,1)S(1)}, bf16[180,360]{1,0:T(8,128)(2,1)}, u32[]{:S(2)}) copy-start(bf16[180,360]{1,0:T(8,128)(2,1)} %param.22) | copy-start | bytes 388804
  57.9 13.7 %copy-start.7 = (f32[180]{0:T(256)S(1)}, f32[180]{0:T(256)}, u32[]{:S(2)}) copy-start(f32[180]{0:T(256)} %param.21) | copy-start | bytes 2164
  57.9 100.0 %all-to-all-start.1 = ((bf16[64,180,128]{2,1,0:T(8,128)(2,1)}), bf16[64,180,128]{2,1,0:T(8,128)(2,1)S(1)}, u32[]{:S(2)}, u32[]{:S(2)}) async-start(bf16[64,180,128]{2,1,0:T(8,128)(2,1)} %scatter_fusion), calls=%async_computation.1 | async-start | bytes 6029312 | tf_op jit(solution)/shard_map/all_to_all | solution.py:250
  82.7 70.7 %collective-permute-start.1 = (bf16[4,256,180]{2,1,0:T(8,128)(2,1)}, bf16[4,256,180]{2,1,0:T(8,128)(2,1)S(1)}, u32[]{:S(2)}, u32[]{:S(2)}) collective-permute-start(bf16[4,256,180]{2,1,0:T(8,128)(2,1)} %get-tuple-element.4), channel_id=1, source_target_pairs={{0,4},{4,8},{8,12},{12,16},{16,20},{20,24},{24,28},{28,32},{32,36}... | collective-permute-start | bytes 1105928 | tf_op jit(solution)/shard_map/ppermute | solution.py:27

commit v2 on v1

--- a/solution.py
+++ b/solution.py
@@ -1,5 +1,3 @@
-import functools
-
 import jax
 import jax.numpy as jnp
 from jax import lax
@@ -17,7 +15,12 @@
 LANES = TILE * TOKENS
 SHIFT = 4
 CAP = 8
+ROWS_PAD = 184
+X_SIZE = 4
+Z_SIZE = 8
+Y_SIZE = 2
 EPSILON = 1e-05
+MESH = pl.DeviceIdType.MESH
 VMEM_LIMIT = 60 << 20
 
 
@@ -45,8 +48,14 @@
     return jnp.concatenate([looked, looked], axis=2)
 
 
+def clear_pad(values):
+    edge = CHAN - CHAN % 8
+    row = lax.broadcasted_iota(jnp.int32, (ROWS_PAD - edge, LANES), 0)
+    return jnp.concatenate([values[:edge], jnp.where(row < CHAN - edge, values[edge:], 0.0)], axis=0)
+
+
 def norm_columns(values, gain):
-    center = values - jnp.sum(values, axis=0, keepdims=True) * (1.0 / CHAN)
+    center = clear_pad(values - jnp.sum(values, axis=0, keepdims=True) * (1.0 / CHAN))
     spread = jnp.sum(center * center, axis=0, keepdims=True) * (1.0 / CHAN)
     return (center * lax.rsqrt(spread + EPSILON) * gain).astype(jnp.bfloat16)
 
@@ -88,11 +97,11 @@
         mixed.append(jnp.dot(value, spread, preferred_element_type=jnp.float32).astype(jnp.bfloat16))
     mixed = jnp.concatenate(mixed, axis=0)
     projected = jnp.dot(proj_t, mixed, preferred_element_type=jnp.float32)
-    return (x_cols + projected).astype(jnp.bfloat16)
+    return x_cols + projected
 
 
 def feed_tile(state, gain, hidden_t, output_t):
-    state = state.astype(jnp.float32)
+    state = clear_pad(state.astype(jnp.float32))
     normed = norm_columns(state, gain)
     hidden = jnp.dot(hidden_t, normed, preferred_element_type=jnp.float32)
     inner = jax.nn.gelu(hidden).astype(jnp.bfloat16)
@@ -105,7 +114,8 @@
     def one(ref, source, row):
         values = ref[source].astype(jnp.float32)
         values = jnp.concatenate([values[SHIFT:], values[:SHIFT]], axis=0)
-        windows[:, pl.ds(pl.multiple_of(row * WIN, WIN), WIN), :] = values.reshape(count, WIN, CHAN)
+        values = values.reshape(count, WIN, CHAN)
+        windows[:, pl.ds(pl.multiple_of(row * WIN, WIN), WIN), 0:CHAN] = values
 
     for row in range(WIN - SHIFT):
         one(pixels_ref, row + SHIFT, row)
@@ -113,7 +123,7 @@
         one(halo_ref, row, row + WIN - SHIFT)
 
 
-def order_windows(keep_ref, count_ref, order):
+def order_windows(keep_ref, count_ref, order, source_ref):
     total = order.shape[0] - 1
     for place in range(total + 1):
         order[place] = total
@@ -122,6 +132,7 @@
         kept = keep_ref[index]
         live = jnp.logical_and(kept == 1, position < count_ref[0])
         order[jnp.where(live, position, total)] = index
+        source_ref[index] = jnp.where(live, position + total, index)
         return position + kept
 
     lax.fori_loop(0, total, step, jnp.int32(0))
@@ -141,47 +152,278 @@
 
 
 def attend_kernel(
-    keep_ref, count_ref, band_ref, pixels_ref, halo_ref, gain_ref, qkv_ref, proj_ref, bias_ref, out_ref, windows, order
+    keep_ref,
+    count_ref,
+    dest_ref,
+    slot_ref,
+    band_ref,
+    pixels_ref,
+    halo_ref,
+    gain_ref,
+    qkv_ref,
+    proj_ref,
+    bias_ref,
+    out_ref,
+    held_ref,
+    source_ref,
+    windows,
+    order,
 ):
     total = windows.shape[0] - 1
+    tiles = out_ref.shape[0] - 1
+    bands = held_ref.shape[0] - 1
+    windows[:, :, CHAN:] = jnp.zeros((total + 1, TOKENS, ROWS_PAD - CHAN), jnp.float32)
     load_windows(pixels_ref, halo_ref, windows.at[pl.ds(0, total)])
-    windows[total] = jnp.zeros((TOKENS, CHAN), jnp.float32)
-    order_windows(keep_ref, count_ref, order)
+    windows[total] = jnp.zeros((TOKENS, ROWS_PAD), jnp.float32)
+    order_windows(keep_ref, count_ref, order, source_ref)
+    for band in range(bands + 1):
+        held_ref[band] = tiles
+    row = lax.broadcasted_iota(jnp.int32, (ROWS_PAD, LANES), 0)
 
     def step(tile, carry):
+        slot = slot_ref[tile]
+        live = jnp.logical_and(tile * TILE < count_ref[0], slot < CAP)
+        held_ref[jnp.where(live, dest_ref[tile], bands)] = tile
         one = order[tile * TILE]
         two = order[tile * TILE + 1]
         x_cols = jnp.concatenate([windows[one], windows[two]], axis=0).T
         mask = region_mask(
             band_ref[0], (one == total - 1).astype(jnp.int32), (two == total - 1).astype(jnp.int32)
         )
-        out_ref[tile] = attend_tile(x_cols, mask, gain_ref[...], qkv_ref[...], proj_ref[...], bias_ref)
+        done = attend_tile(x_cols, mask, gain_ref[...], qkv_ref[...], proj_ref[...], bias_ref)
+        out_ref[tile] = jnp.where(row < CHAN, done, slot.astype(jnp.float32)).astype(jnp.bfloat16)
         return carry
 
-    lax.fori_loop(0, out_ref.shape[0], step, 0, unroll=2)
-
-
-def feed_kernel(
-    keep_ref, count_ref, pixels_ref, halo_ref, state_ref, gain_ref, hidden_ref, output_ref, own_ref, sent_ref, windows, order
+    lax.fori_loop(0, tiles, step, 0, unroll=2)
+    out_ref[tiles] = jnp.where(row < CHAN, 0.0, float(CAP)).astype(jnp.bfloat16)
+    held_ref[bands] = tiles
+
+
+def band_of(x, z, y):
+    return (lax.rem(x, X_SIZE) * Z_SIZE + lax.rem(z, Z_SIZE)) * Y_SIZE + lax.rem(y, Y_SIZE)
+
+
+def exchange_kernel(
+    held_ref,
+    source_ref,
+    pixels_ref,
+    halo_ref,
+    state_ref,
+    gain_ref,
+    hidden_ref,
+    output_ref,
+    restored_ref,
+    work_ref,
+    pool,
+    windows,
+    sent_rows,
+    got_rows,
+    y_out,
+    x_out,
+    x_in,
+    z_out,
+    z_in,
+    total_ref,
+    rows_sem,
+    y_sem,
+    x_sem,
+    z_sem,
 ):
-    total = windows.shape[0] - 1
-    load_windows(pixels_ref, halo_ref, windows.at[pl.ds(0, total)])
-    order_windows(keep_ref, count_ref, order)
-
-    def step(tile, carry):
-        done = feed_tile(state_ref[tile], gain_ref[...], hidden_ref[...], output_ref[...]).T
-        windows[order[tile * TILE]] = done[:TOKENS]
-        windows[order[tile * TILE + 1]] = done[TOKENS:]
+    me = lax.axis_index("band")
+    bands = lax.axis_size("band")
+    x = me // (Z_SIZE * Y_SIZE)
+    z = lax.rem(me // Y_SIZE, Z_SIZE)
+    y = lax.rem(me, Y_SIZE)
+    x_peers = [band_of(x + step, z, y) for step in range(1, X_SIZE)]
+    y_peer = band_of(x, z, y + 1)
+    z_peers = [band_of(x, z + 1, y), band_of(x, z + Z_SIZE - 1, y)]
+    after = lax.rem(me + 1, bands)
+    before = lax.rem(me + bands - 1, bands)
+    barrier = pltpu.get_barrier_semaphore()
+    greeted = x_peers + [y_peer] + z_peers + [after, before]
+    for peer in greeted:
+        pl.semaphore_signal(barrier, inc=1, device_id={"band": peer}, device_id_type=MESH)
+
+    far = Z_SIZE // 2
+    order = [far]
+    for away in range(far - 1, 0, -1):
+        order += [away, Z_SIZE - away]
+    order += [0]
+
+    def stage(away):
+        def step(ahead, carry):
+            y_out[away, ahead] = state_ref[held_ref[band_of(x + ahead, z + away, y + 1)]]
+            x_out[away, 0, ahead] = state_ref[held_ref[band_of(x + ahead, z + away, y)]]
+            return carry
+
+        lax.fori_loop(0, X_SIZE, step, 0)
+
+    def copy(source, target, sems, index, peer):
+        return pltpu.make_async_remote_copy(
+            src_ref=source,
+            dst_ref=target,
+            send_sem=sems.at[(0,) + index],
+            recv_sem=sems.at[(1,) + index],
+            device_id={"band": peer},
+            device_id_type=MESH,
+        )
+
+    def y_copy(away):
+        return copy(y_out.at[away], x_out.at[away, 1], y_sem, (away,), y_peer)
+
+    def x_copy(away, ahead):
+        return copy(
+            x_out.at[away, :, ahead], x_in.at[away, ahead - 1], x_sem, (away, ahead - 1), x_peers[ahead - 1]
+        )
+
+    half = CAP // 2
+
+    def z_copy(side, hop, part):
+        piece = pl.ds(part * half, half)
+        return copy(
+            z_out.at[side, hop, piece], z_in.at[side, hop, piece], z_sem, (side, hop, part), z_peers[side]
+        )
+
+    def pass_x(away):
+        y_copy(away).wait_recv()
+        for ahead in range(1, X_SIZE):
+            x_copy(away, ahead).start()
+
+    def wait_x(away):
+        for ahead in range(1, X_SIZE):
+            x_copy(away, ahead).wait_recv()
+
+    def gather(away, part, target, arrived):
+        found = [x_out.at[away, 0, 0], x_out.at[away, 1, 0]]
+        for ahead in range(X_SIZE - 1):
+            found += [x_in.at[away, ahead, 0], x_in.at[away, ahead, 1]]
+
+        def step(index, carry):
+            slot = part * half + index
+            number = slot.astype(jnp.float32)
+            sum_ = None if arrived is None else arrived[slot]
+            for one in found:
+                mark = one[CHAN : CHAN + 1, :].astype(jnp.float32)
+                term = one[...] * jnp.where(mark == number, 1.0, 0.0).astype(jnp.bfloat16)
+                sum_ = term if sum_ is None else sum_ + term
+            target[slot] = sum_
+            return carry
+
+        lax.fori_loop(0, half, step, 0)
+
+    fed = [0]
+
+    def feed(count):
+        start = fed[0]
+
+        def step(tile, carry):
+            done = feed_tile(state_ref[tile], gain_ref[...], hidden_ref[...], output_ref[...]).T
+            base = window_total + tile * TILE
+            pool[base] = done[:TOKENS, :CHAN]
+            pool[base + 1] = done[TOKENS:, :CHAN]
+            return carry
+
+        lax.fori_loop(start, start + count, step, 0, unroll=min(count, 2))
+        fed[0] = start + count
+
+    window_total = source_ref.shape[0]
+    tiles = state_ref.shape[0] - 1
+    share = tiles // 8
+
+    for away in order:
+        stage(away)
+    pl.semaphore_wait(barrier, len(greeted))
+    for away in order:
+        y_copy(away).start()
+    load_windows(pixels_ref, halo_ref, pool.at[pl.ds(0, window_total)])
+
+    def hop_far():
+        wait_x(far)
+        for side in range(2):
+            gather(far, side, z_out.at[side, 0], None)
+            z_copy(side, 0, side).start()
+
+    def hop(side, number):
+        away = far - number if side == 0 else Z_SIZE - far + number
+        wait_x(away)
+        parts = (1 - side, side) if number == 1 else (0, 1)
+        for part in parts:
+            if number == 1 and part != side:
+                arrived = None
+            else:
+                z_copy(side, number - 1, part).wait_recv()
+                arrived = z_in.at[side, number - 1]
+            gather(away, part, z_out.at[side, number], arrived)
+            z_copy(side, number, part).start()
+
+    def rows_copy():
+        return copy(sent_rows, got_rows, rows_sem, (), after)
+
+    def rows(first, count, target):
+        for row in range(count):
+            at = (first + row) * WIN
+            values = windows[:, at : at + WIN, :].reshape(window_total * WIN, CHAN)
+            values = jnp.concatenate([values[-SHIFT:], values[:-SHIFT]], axis=0)
+            target[row] = values.astype(jnp.bfloat16)
+
+    pass_x(order[0])
+    feed(share)
+    pass_x(order[1])
+    pass_x(order[2])
+    feed(share)
+    hop_far()
+    feed(share)
+    pass_x(order[3])
+    pass_x(order[4])
+    feed(share)
+    hop(0, 1)
+    feed(share)
+    hop(1, 1)
+    pass_x(order[5])
+    pass_x(order[6])
+    feed(share)
+    hop(0, 2)
+    feed(share)
+    hop(1, 2)
+    pass_x(order[7])
+    feed(tiles - fed[0])
+
+    def move(window, carry):
+        windows[window] = pool[source_ref[window]]
         return carry
 
-    lax.fori_loop(0, state_ref.shape[0], step, 0, unroll=2)
-    for row in range(WIN):
-        values = windows[0:total, row * WIN : (row + 1) * WIN, :].reshape(total * WIN, CHAN)
-        values = jnp.concatenate([values[-SHIFT:], values[:-SHIFT]], axis=0).astype(jnp.bfloat16)
-        if row < WIN - SHIFT:
-            own_ref[row] = values
-        else:
-            sent_ref[row - WIN + SHIFT] = values
+    lax.fori_loop(0, window_total, move, 0)
+    rows(WIN - SHIFT, SHIFT, sent_rows)
+    rows_copy().start()
+    hop(0, 3)
+    hop(1, 3)
+    rows(0, WIN - SHIFT, restored_ref.at[pl.ds(SHIFT, WIN - SHIFT)])
+    wait_x(0)
+    for part in range(2):
+        gather(0, part, total_ref, None)
+    rows_copy().wait_recv()
+    restored_ref[0:SHIFT] = got_rows[...]
+    for part in range(2):
+        for side in range(2):
+            z_copy(side, far - 1, part).wait_recv()
+
+        def finish(index, carry):
+            slot = part * half + index
+            values = total_ref[slot] + z_in[0, far - 1, slot] + z_in[1, far - 1, slot]
+            work_ref[slot] = values.astype(jnp.float32).T[:, :CHAN].astype(jnp.bfloat16)
+            return carry
+
+        lax.fori_loop(0, half, finish, 0)
+    for away in order:
+        y_copy(away).wait_send()
+        for ahead in range(1, X_SIZE):
+            x_copy(away, ahead).wait_send()
+    for side in range(2):
+        z_copy(side, 0, side).wait_send()
+        for number in range(1, far):
+            for part in range(2):
+                z_copy(side, number, part).wait_send()
+    rows_copy().wait_send()
 
 
 def pad_heads(weight):
@@ -213,18 +455,21 @@
     row_count, col_count, channels = pixels.shape
     window_total = keep_mask.shape[1]
     tile_total = window_total // TILE
-    tile_tokens = TILE * TOKENS
     halo = from_behind(pixels[:SHIFT], "band", -1)
     last_band = (band_index == band_total - 1).astype(jnp.int32).reshape(1)
     keep = keep_mask.reshape(window_total)
-    kept_count = band_counts[0]
-    attended = pl.pallas_call(
+    pad = ROWS_PAD - CHAN
+    tiles, held, source = pl.pallas_call(
         attend_kernel,
-        out_shape=jax.ShapeDtypeStruct((tile_total, CHAN, LANES), jnp.bfloat16),
-        in_specs=[SMEM] * 3 + [VMEM] * 6,
-        out_specs=VMEM,
+        out_shape=[
+            jax.ShapeDtypeStruct((tile_total + 1, ROWS_PAD, LANES), jnp.bfloat16),
+            jax.ShapeDtypeStruct((band_total + 1,), jnp.int32),
+            jax.ShapeDtypeStruct((window_total,), jnp.int32),
+        ],
+        in_specs=[SMEM] * 5 + [VMEM] * 6,
+        out_specs=[VMEM, SMEM, SMEM],
         scratch_shapes=[
-            pltpu.VMEM((window_total + 1, TOKENS, CHAN), jnp.float32),
+            pltpu.VMEM((window_total + 1, TOKENS, ROWS_PAD), jnp.float32),
             pltpu.SMEM((window_total + 1,), jnp.int32),
         ],
         compiler_params=pltpu.CompilerParams(vmem_limit_bytes=VMEM_LIMIT),
@@ -233,54 +478,57 @@
     )(
         keep,
         band_counts,
+        plan_dest.reshape(-1),
+        plan_slot.reshape(-1),
         last_band,
         pixels,
         halo,
-        gain_attn.reshape(CHAN, 1),
-        pad_heads(qkv_weight).T,
-        pad_heads(proj_weight.T),
+        jnp.pad(gain_attn, (0, pad)).reshape(ROWS_PAD, 1),
+        jnp.pad(pad_heads(qkv_weight), ((0, pad), (0, 0))).T,
+        jnp.pad(pad_heads(proj_weight.T), ((0, pad), (0, 0))),
         position_bias(bias_table),
     )
-    tile_ids = jnp.arange(tile_total, dtype=jnp.int32)
-    tile_live = tile_ids * TILE < kept_count
-    destinations = plan_dest[0]
-    sent_slot = jnp.where(tile_live, plan_slot[0], CAP).astype(jnp.bfloat16)
-    outgoing_slots = jnp.full((band_total, 1), CAP, jnp.bfloat16).at[destinations, 0].set(sent_slot)
-    outgoing = jnp.zeros((band_total, CHAN, LANES), jnp.bfloat16).at[destinations].set(attended)
-    incoming = lax.all_to_all(outgoing, "band", split_axis=0, concat_axis=0, tiled=True)
-    incoming_slots = lax.all_to_all(outgoing_slots, "band", split_axis=0, concat_axis=0, tiled=True)
-    own, sent = pl.pallas_call(
-        feed_kernel,
+    tile_shape = (ROWS_PAD, LANES)
+    far = Z_SIZE // 2
+    restored, work = pl.pallas_call(
+        exchange_kernel,
         out_shape=[
-            jax.ShapeDtypeStruct((row_count - SHIFT, col_count, CHAN), jnp.bfloat16),
-            jax.ShapeDtypeStruct((SHIFT, col_count, CHAN), jnp.bfloat16),
+            jax.ShapeDtypeStruct((row_count, col_count, CHAN), jnp.bfloat16),
+            jax.ShapeDtypeStruct((CAP, LANES, CHAN), jnp.bfloat16),
         ],
         in_specs=[SMEM] * 2 + [VMEM] * 6,
         out_specs=[VMEM, VMEM],
         scratch_shapes=[
-            pltpu.VMEM((window_total + 1, TOKENS, CHAN), jnp.float32),
-            pltpu.SMEM((window_total + 1,), jnp.int32),
+            pltpu.VMEM((2 * window_total, TOKENS, CHAN), jnp.float32),
+            pltpu.VMEM((window_total, TOKENS, CHAN), jnp.float32),
+            pltpu.VMEM((SHIFT, col_count, CHAN), jnp.bfloat16),
+            pltpu.VMEM((SHIFT, col_count, CHAN), jnp.bfloat16),
+            pltpu.VMEM((Z_SIZE, X_SIZE) + tile_shape, jnp.bfloat16),
+            pltpu.VMEM((Z_SIZE, Y_SIZE, X_SIZE) + tile_shape, jnp.bfloat16),
+            pltpu.VMEM((Z_SIZE, X_SIZE - 1, Y_SIZE) + tile_shape, jnp.bfloat16),
+            pltpu.VMEM((2, far, CAP) + tile_shape, jnp.bfloat16),
+            pltpu.VMEM((2, far, CAP) + tile_shape, jnp.bfloat16),
+            pltpu.VMEM((CAP,) + tile_shape, jnp.bfloat16),
+            pltpu.SemaphoreType.DMA((2,)),
+            pltpu.SemaphoreType.DMA((2, Z_SIZE)),
+            pltpu.SemaphoreType.DMA((2, Z_SIZE, X_SIZE - 1)),
+            pltpu.SemaphoreType.DMA((2, 2, far, 2)),
         ],
-        compiler_params=pltpu.CompilerParams(vmem_limit_bytes=VMEM_LIMIT),
+        compiler_params=pltpu.CompilerParams(
+            vmem_limit_bytes=VMEM_LIMIT, collective_id=0, has_side_effects=True
+        ),
         cost_estimate=pl.CostEstimate(flops=2 * 10**9, bytes_accessed=2 * 10**6, transcendentals=10**6),
-        name="feed",
+        name="exchange",
     )(
-        keep,
-        band_counts,
+        held,
+        source,
         pixels,
         halo,
-        attended,
-        gain_mlp.reshape(CHAN, 1),
-        hidden_weight.T,
-        output_weight.T,
+        tiles,
+        jnp.pad(gain_mlp, (0, pad)).reshape(ROWS_PAD, 1),
+        jnp.pad(hidden_weight, ((0, pad), (0, 0))).T,
+        jnp.pad(output_weight, ((0, 0), (0, pad))).T,
     )
-    arrived_slot = incoming_slots.reshape(-1).astype(jnp.int32)
-    work = (
-        jnp.zeros((CAP, CHAN, LANES), jnp.bfloat16).at[arrived_slot].set(incoming, mode="drop")
-    )
-    work = jnp.transpose(work, (0, 2, 1))
-    upper_rows = from_behind(sent, "band", 1)
-    restored = jnp.concatenate([upper_rows, own], axis=0)
     return (restored, work)
 
 

time: 164 us -> 124 us (0.76)
  waiting for transfers between devices: 66.4 us -> 3.14 us
  Pallas kernels: 37 us -> 95.3 us
  starting transfers between devices: 31 us -> 9.86 us
  local copies, waits for them, and re-layouts: 20.2 us -> 10.9 us
  other arithmetic: 5.62 us -> 0.89 us
    ppermute x2 -> x1, waiting for transfers between devices: 66.4 us -> 3.14 us  [from_behind(): return lax.ppermute(value, axis, pairs)]
    pallas_call x2, Pallas kernels: 37 us -> 95.3 us  [the longest x1 68.4 us: shards(): pl.pallas_call(exchange_kernel, out_shape=[jax.ShapeDtypeStruct((row_coun...]
    all_to_all x2 -> x0, starting transfers between devices: 18 us -> none  [the longest x1 12.9 us: shards(): lax.all_to_all(outgoing, 'band', split_axis=0, concat_axis=0, tiled=True)]
    scatter x3 -> x0, local copies, waits for them, and re-layouts: 7.54 us -> none  [the longest x1 4.13 us: shards(): jnp.zeros((CAP, CHAN, LANES), jnp.bfloat16).at[arrived_slot]]
    unnamed x23, local copies, waits for them, and re-layouts: 6.48 us -> 2.67 us
    pallas_call x0 -> x2, local copies, waits for them, and re-layouts: none -> 3.37 us  [shards(): pl.pallas_call(exchange_kernel, out_shape=[jax.ShapeDtypeStruct((row_coun...]
    ppermute x2 -> x1, starting transfers between devices: 12.9 us -> 9.86 us  [from_behind(): return lax.ppermute(value, axis, pairs)]
    concatenate x2 -> x0, other arithmetic: 2.86 us -> none  [the longest x1 2.2 us: shards(): restored = jnp.concatenate([upper_rows, own], axis=0)]
  transfers between devices with their start and end apart: 4 -> 1, of which waited for: 1 -> 1; matrix products, arithmetic and copies ran while one was open for 12% -> 6% of each run, Pallas kernels for 23% -> 0%
where the time goes in v2:
time: 124 us; the launch traced here: 123 us
  Pallas kernels  95.3 us (77%)
  local copies, waits for them, and re-layouts  10.9 us (9%)
  starting transfers between devices  9.86 us (8%)
  waiting for transfers between devices  3.14 us (3%)
  between operations  1.47 us (1%)
  matrix products  1.3 us (1%)
    pallas_call x1, Pallas kernels, shards(): pl.pallas_call(exchange_kernel, out_shape=[jax.ShapeDtypeStruct((row_coun...  68.4 us
    pallas_call x1, Pallas kernels, shards(): pl.pallas_call(attend_kernel, out_shape=[jax.ShapeDtypeStruct((tile_total...  26.8 us
    ppermute x1, starting transfers between devices, from_behind(): return lax.ppermute(value, axis, pairs)  9.86 us
    pallas_call x2, local copies, waits for them, and re-layouts, shards(): pl.pallas_call(exchange_kernel, out_shape=[jax.ShapeDtypeStruct((row_coun...  3.37 us
    ppermute x1, waiting for transfers between devices, from_behind(): return lax.ppermute(value, axis, pairs)  3.14 us
    unnamed x23, local copies, waits for them, and re-layouts  2.67 us
  transfers between devices with their start and end apart: 1, of which 1 were waited for; matrix products, arithmetic and copies ran while one was open for 6% of the time, Pallas kernels for 0%

profile of v2, /device:TPU:8, one launch (start us, length us, event | category | flops | bytes accessed | tf_op | source)
XLA Modules:
  0.0 122.8 jit_solution(1484801138099917372)
XLA Ops:
  0.6 0.0 copy-start
  0.6 1.5 %copy.25.pixels_ref = bf16[8,256,180]{2,1,0:T(8,128)(2,1)S(1)} copy(bf16[8,256,180]{1,0,2:T(8,128)(2,1)} %param.12) | data formatting | bytes 1474560 | tf_op args[0]
  2.2 0.0 copy-start.1
  2.2 0.0 copy-start.4
  2.2 0.0 copy-start.7
  2.2 0.0 copy-start.8
  2.2 0.0 copy-start.6
  2.3 9.9 %collective-permute-start = (bf16[4,256,180]{2,1,0:T(8,128)(2,1)S(1)}, bf16[4,256,180]{2,1,0:T(8,128)(2,1)S(1)}, u32[]{:S(2)}, u32[]{:S(2)}) collective-permute-start(bf16[4,256,180]{2,1,0:T(8,128)(2,1)S(1)} %slice.4), channel_id=1, source_target_pairs={{0,252},{4,0},{8,4},{12,8},{16,12},{20,16},{24,20},{28,24},{32,28}... | collective-permute-start | bytes 1105928 | tf_op jit(solution)/shard_map/ppermute | solution.py:30
  12.2 0.1 add_add_fusion
  12.2 0.1 add.71
  12.3 0.0 copy-done
  12.3 1.3 %convolution_bitcast_fusion = f32[6,4096]{1,0:T(8,128)S(1)} fusion(f32[225,6]{0,1:T(8,128)S(1)} %copy-done, s32[4096]{0:T(1024)S(1)} %add.71), kind=kOutput, calls=%fused_computation | convolution fusion | flops 67276800 | bytes 120088 | tf_op jit(solution)/shard_map/dot_general | solution.py:44
  13.6 0.7 pad_bitcast_fusion.2.output_ref
  15.0 0.8 copy.29.gain_ref
  15.8 0.8 copy.26.gain_ref
  16.6 0.1 copy.24
  16.7 0.7 pad.35.proj_ref
  17.4 0.1 reshape.133
  17.5 0.1 copy.27
  17.6 0.2 copy.23
  17.8 0.1 reshape.129
  17.9 0.1 pad.32
  17.9 0.7 pad_bitcast_fusion.1.hidden_ref
  18.6 0.8 pad_maximum_fusion.bias_ref
  19.4 0.8 pad_bitcast_fusion.qkv_ref
  20.2 3.1 %collective-permute-done.halo_ref = bf16[4,256,180]{2,1,0:T(8,128)(2,1)S(1)} collective-permute-done((bf16[4,256,180]{2,1,0:T(8,128)(2,1)S(1)}, bf16[4,256,180]{2,1,0:T(8,128)(2,1)S(1)}, u32[]{:S(2)}, u32[]{:S(2)}) %collective-permute-start) | collective-permute-done | bytes 368672 | tf_op jit(solution)/shard_map/ppermute | solution.py:30
  23.3 0.8 copy-done.9
  24.1 26.8 %attend.1 = (bf16[17,184,128]{2,1,0:T(8,128)(2,1)}, s32[65]{0:T(128)}, s32[32]{0:T(128)}) custom-call(s32[32]{0:T(128)} %bitcast.27, s32[1]{0:T(128)S(6)} %copy.32.count_ref, s32[16]{0:T(128)} %bitcast.28, s32[16]{0:T(128)} %bitcast.29, s32[1]{0:T(128)} %bitcast.3.band_ref, bf16[8,256,180]{2,1,0:T(8,128)(2,1)} %copy-done.1, bf16[4,256,180]{2,1,0:T(8,128)(2,1)} %copy-done.9, ...), custom_call_target="tpu_custom_call" | custom-call | flops 2000000000 | bytes 2000000 | tf_op jit(solution)/shard_map/attend/pallas_call | solution.py:462
  51.0 68.4 %exchange.1 = (bf16[8,256,180]{2,1,0:T(8,128)(2,1)}, bf16[8,128,180]{2,1,0:T(8,128)(2,1)}) custom-call(s32[65]{0:T(128)} %get-tuple-element.5.held_ref, s32[32]{0:T(128)} %get-tuple-element.6.source_ref, bf16[8,256,180]{2,1,0:T(8,128)(2,1)} %copy-done.1, bf16[4,256,180]{2,1,0:T(8,128)(2,1)} %copy-done.9, bf16[17,184,128]{2,1,0:T(8,128)(2,1)} %get-tuple-element.7.state_ref, ...), custom_call_target="tpu_custom_call" | custom-call | flops 2000000000 | bytes 2000000 | tf_op jit(solution)/shard_map/exchange/pallas_call | solution.py:493
  119.4 0.0 copy-start.2
  119.4 2.4 %copy.30 = bf16[8,256,180]{1,0,2:T(8,128)(2,1)} copy(bf16[8,256,180]{2,1,0:T(8,128)(2,1)} %get-tuple-element.10) | data formatting | bytes 1474560 | tf_op jit(solution)/shard_map/exchange/pallas_call | solution.py:493
  121.8 1.0 copy.31
  (17 shorter events, 0.1 us)
Async XLA Ops:
  0.6 11.7 %copy-start = (f32[225,6]{0,1:T(8,128)S(1)}, f32[225,6]{0,1:T(8,128)}, u32[]{:S(2)}) copy-start(f32[225,6]{0,1:T(8,128)} %param.17) | copy-start | bytes 16204
  2.2 12.1 %copy-start.1 = (bf16[8,256,180]{2,1,0:T(8,128)(2,1)}, bf16[8,256,180]{2,1,0:T(8,128)(2,1)S(1)}, u32[]{:S(2)}) copy-start(bf16[8,256,180]{2,1,0:T(8,128)(2,1)S(1)} %copy.25.pixels_ref) | copy-start | bytes 2211844
  2.2 11.4 %copy-start.4 = (bf16[360,180]{0,1:T(8,128)(2,1)S(1)}, bf16[360,180]{0,1:T(8,128)(2,1)}, u32[]{:S(2)}) copy-start(bf16[360,180]{0,1:T(8,128)(2,1)} %param.23) | copy-start | bytes 388804
  2.2 12.7 %copy-start.7 = (f32[180]{0:T(256)S(1)}, f32[180]{0:T(256)}, u32[]{:S(2)}) copy-start(f32[180]{0:T(256)} %param.18) | copy-start | bytes 2164
  2.2 12.8 %copy-start.8 = (f32[180]{0:T(256)S(1)}, f32[180]{0:T(256)}, u32[]{:S(2)}) copy-start(f32[180]{0:T(256)} %param.21) | copy-start | bytes 2164
  2.2 14.3 %copy-start.6 = (bf16[180,180]{1,0:T(8,128)(2,1)S(1)}, bf16[180,180]{1,0:T(8,128)(2,1)}, u32[]{:S(2)}) copy-start(bf16[180,180]{1,0:T(8,128)(2,1)} %param.20) | copy-start | bytes 194404
  2.3 21.0 %collective-permute-start = (bf16[4,256,180]{2,1,0:T(8,128)(2,1)S(1)}, bf16[4,256,180]{2,1,0:T(8,128)(2,1)S(1)}, u32[]{:S(2)}, u32[]{:S(2)}) collective-permute-start(bf16[4,256,180]{2,1,0:T(8,128)(2,1)S(1)} %slice.4), channel_id=1, source_target_pairs={{0,252},{4,0},{8,4},{12,8},{16,12},{20,16},{24,20},{28,24},{32,28}... | collective-permute-start | bytes 1105928 | tf_op jit(solution)/shard_map/ppermute | solution.py:30
  12.3 5.1 %copy-start.5 = (bf16[180,360]{1,0:T(8,128)(2,1)S(1)}, bf16[180,360]{1,0:T(8,128)(2,1)}, u32[]{:S(2)}) copy-start(bf16[180,360]{1,0:T(8,128)(2,1)} %param.22) | copy-start | bytes 388804
  13.6 4.0 %copy-start.3 = (bf16[180,540]{1,0:T(8,128)(2,1)S(1)}, bf16[180,540]{1,0:T(8,128)(2,1)}, u32[]{:S(2)}) copy-start(bf16[180,540]{1,0:T(8,128)(2,1)} %param.19) | copy-start | bytes 583204
  23.3 0.8 copy-start.9
  119.4 2.4 %copy-start.2 = (bf16[8,128,180]{2,1,0:T(8,128)(2,1)S(1)}, bf16[8,128,180]{2,1,0:T(8,128)(2,1)}, u32[]{:S(2)}) copy-start(bf16[8,128,180]{2,1,0:T(8,128)(2,1)} %get-tuple-element.11) | copy-start | bytes 1105924

commit v3 on v2

v3 whole, which is shorter than its diff:
```python
import jax
import jax.numpy as jnp
from jax import lax
from jax.experimental import pallas as pl
from jax.experimental.pallas import tpu as pltpu
from jax.sharding import PartitionSpec as P

CHAN = 180
FF_WIDTH = 360
HEADS = 6
HEAD_DIM = CHAN // HEADS
HEAD_PAD = 32
WIN = 8
TOKENS = WIN * WIN
TILE = 2
LANES = TILE * TOKENS
SHIFT = 4
CAP = 8
ROWS_PAD = 184
X_SIZE = 4
Z_SIZE = 8
Y_SIZE = 2
EPSILON = 1e-05
MESH = pl.DeviceIdType.MESH
VMEM_LIMIT = 60 << 20


def norm_columns(values, gain):
    center = values - jnp.sum(values, axis=0, keepdims=True) * (1.0 / CHAN)
    spread = jnp.sum(center * center, axis=0, keepdims=True) * (1.0 / CHAN)
    return (center * lax.rsqrt(spread + EPSILON) * gain).astype(jnp.bfloat16)


def split_two(values):
    high = values.astype(jnp.bfloat16)
    low = (values - high.astype(jnp.float32)).astype(jnp.bfloat16)
    return high, low


def attend_tile(x_cols, mask, gain, qkv_t, proj_t, bias_ref):
    lane = lax.broadcasted_iota(jnp.int32, (TOKENS, LANES), 1)
    first = lane < TOKENS
    normed = norm_columns(x_cols, gain)
    qkv = jnp.dot(qkv_t, normed, preferred_element_type=jnp.float32)
    mixed = []
    width = HEADS * HEAD_PAD
    for head in range(HEADS):
        at = head * HEAD_PAD
        query = qkv[at : at + HEAD_PAD] * HEAD_DIM ** (-0.5)
        key = qkv[width + at : width + at + HEAD_PAD]
        value = qkv[2 * width + at : 2 * width + at + HEAD_PAD].astype(jnp.bfloat16)
        query_high, query_low = split_two(query)
        key_high, key_low = split_two(key)
        left = jnp.concatenate([key_high, key_low, key_high], axis=0)
        right = jnp.concatenate([query_high, query_high, query_low], axis=0)
        full = lax.dot_general(
            left, right, (((0,), (0,)), ((), ())), preferred_element_type=jnp.float32
        )
        scores = jnp.where(first, full[:TOKENS], full[TOKENS:])
        scores = (scores + bias_ref[head]) + mask
        top = jnp.max(scores, axis=0, keepdims=True)
        grown = jnp.exp(scores - top)
        total = jnp.sum(grown, axis=0, keepdims=True)
        weights = grown * (1.0 / total)
        spread = jnp.concatenate(
            [jnp.where(first, weights, 0.0), jnp.where(first, 0.0, weights)], axis=0
        ).astype(jnp.bfloat16)
        mixed.append(jnp.dot(value, spread, preferred_element_type=jnp.float32).astype(jnp.bfloat16))
    mixed = jnp.concatenate(mixed, axis=0)
    projected = jnp.dot(proj_t, mixed, preferred_element_type=jnp.float32)
    return (x_cols + projected).astype(jnp.bfloat16)


def feed_tile(state, gain, hidden_t, output_t):
    state = state.astype(jnp.float32)
    normed = norm_columns(state, gain)
    hidden = jnp.dot(hidden_t, normed, preferred_element_type=jnp.float32)
    inner = jax.nn.gelu(hidden).astype(jnp.bfloat16)
    return state + jnp.dot(output_t, inner, preferred_element_type=jnp.float32)


def iota(shape, dim):
    return lax.broadcasted_iota(jnp.int32, shape, dim)


def region_mask(rows_split, cols_split):
    key = iota((TOKENS, LANES), 0)
    query = iota((TOKENS, LANES), 1) & (TOKENS - 1)
    rows_differ = ((key ^ query) & (SHIFT * WIN)) != 0
    cols_differ = ((key ^ query) & SHIFT) != 0
    row_part = jnp.where(rows_differ, rows_split, 0)
    col_part = jnp.where(cols_differ, cols_split, 0)
    return jnp.where((row_part | col_part) != 0, -100.0, 0.0)


def head_columns(count):
    row = iota((count * HEAD_PAD, count * HEAD_DIM), 0)
    col = iota((count * HEAD_PAD, count * HEAD_DIM), 1)
    inside = row & (HEAD_PAD - 1)
    want = (row >> 5) * HEAD_DIM + inside
    hit = jnp.logical_and(inside < HEAD_DIM, col == want)
    return jnp.where(hit, 1.0, 0.0).astype(jnp.bfloat16)


def build_bias(table_ref, bias_ref):
    span = 2 * WIN - 1
    entries = table_ref.shape[1]
    entry = iota((entries, WIN * LANES), 0)
    lane = iota((entries, WIN * LANES), 1)
    key_col = lane >> 7
    place = lane & (LANES - 1)
    want = (place >> 3) * span + (place & (WIN - 1)) - key_col + WIN - 1
    onehot = jnp.where(entry == want, 1.0, 0.0)
    looked = jnp.dot(
        table_ref[...], onehot, precision=lax.Precision.HIGHEST, preferred_element_type=jnp.float32
    )
    low = iota((HEADS, LANES), 1) < TOKENS
    for col in range(WIN):
        line = looked[:, col * LANES : (col + 1) * LANES]
        for row in range(WIN):
            back = (WIN - 1 - row) * WIN
            moved = line if back == 0 else pltpu.roll(line, LANES - back, 1)
            moved = jnp.where(low, moved, pltpu.roll(moved, TOKENS, 1))
            bias_ref[:, row * WIN + col, :] = moved


def swap_blocks(blocks):
    lane = iota(blocks[0].shape, 1)
    blocks = list(blocks)
    for bit in range(3):
        width = 16 << bit
        low = (lane & width) == 0
        for one in range(8):
            if one & (1 << bit):
                continue
            two = one | (1 << bit)
            first, second = blocks[one], blocks[two]
            blocks[one] = jnp.where(low, first, pltpu.roll(second, width, 1))
            blocks[two] = jnp.where(low, pltpu.roll(first, LANES - width, 1), second)
    return blocks


def shift_lanes(first, second, steps):
    lane = iota(first.shape, 1)
    first, second = pltpu.roll(first, steps % LANES, 1), pltpu.roll(second, steps % LANES, 1)
    own = lane >= steps if steps > 0 else lane < LANES + steps
    return jnp.where(own, first, second), jnp.where(own, second, first)


def plan_kernel(keep_ref, count_ref, dest_ref, slot_ref, order_ref, held_ref, active_ref):
    total = active_ref.shape[0]
    bands = held_ref.shape[0] - 1
    tiles = dest_ref.shape[0]
    for place in range(total + 1):
        order_ref[place] = total
    for band in range(bands + 1):
        held_ref[band] = tiles

    def window_step(index, position):
        kept = keep_ref[index]
        live = jnp.logical_and(kept == 1, position < count_ref[0])
        order_ref[jnp.where(live, position, total)] = index
        active_ref[index] = live.astype(jnp.int32)
        return position + kept

    lax.fori_loop(0, total, window_step, jnp.int32(0))

    def tile_step(tile, carry):
        live = jnp.logical_and(tile * TILE < count_ref[0], slot_ref[tile] < CAP)
        held_ref[jnp.where(live, dest_ref[tile], bands)] = tile
        return carry

    lax.fori_loop(0, tiles, tile_step, 0)


def band_of(x, z, y):
    return (lax.rem(x, X_SIZE) * Z_SIZE + lax.rem(z, Z_SIZE)) * Y_SIZE + lax.rem(y, Y_SIZE)


UNITS = (2, 1, 1, 2, 2, 2, 2, 2, 2)


def block_kernel(
    held_ref,
    order_ref,
    active_ref,
    slot_ref,
    pixels_ref,
    table_ref,
    gain_one_ref,
    qkv_ref,
    proj_ref,
    gain_two_ref,
    hidden_ref,
    output_ref,
    restored_ref,
    work_ref,
    flat,
    mixed,
    natural,
    packed,
    bias,
    qkv_t,
    proj_t,
    hidden_t,
    gains,
    halo_out,
    halo_in,
    rows_out,
    rows_in,
    y_out,
    x_out,
    x_in,
    z_out,
    z_in,
    total_ref,
    done_ref,
    rows_sem,
    y_sem,
    x_sem,
    z_sem,
):
    me = lax.axis_index("band")
    bands = lax.axis_size("band")
    x = me // (Z_SIZE * Y_SIZE)
    z = lax.rem(me // Y_SIZE, Z_SIZE)
    y = lax.rem(me, Y_SIZE)
    x_peers = [band_of(x + step, z, y) for step in range(1, X_SIZE)]
    y_peer = band_of(x, z, y + 1)
    z_peers = [band_of(x, z + 1, y), band_of(x, z + Z_SIZE - 1, y)]
    after = lax.rem(me + 1, bands)
    before = lax.rem(me + bands - 1, bands)
    barrier = pltpu.get_barrier_semaphore()
    greeted = x_peers + [y_peer] + z_peers + [after, before]
    for peer in greeted:
        pl.semaphore_signal(barrier, inc=1, device_id={"band": peer}, device_id_type=MESH)

    blocks = ROWS_PAD // 8
    tiles = packed.shape[0] - 1
    window_total = active_ref.shape[0]
    half = CAP // 2
    far = Z_SIZE // 2
    order = [far]
    for away in range(far - 1, 0, -1):
        order += [away, Z_SIZE - away]
    order += [0]

    def copy(source, target, sems, index, peer):
        return pltpu.make_async_remote_copy(
            src_ref=source,
            dst_ref=target,
            send_sem=sems.at[(0,) + index],
            recv_sem=sems.at[(1,) + index],
            device_id={"band": peer},
            device_id_type=MESH,
        )

    def halo_copy():
        return copy(halo_out, halo_in, rows_sem, (0,), before)

    def rows_copy():
        return copy(rows_out, rows_in, rows_sem, (1,), after)

    def y_copy(away):
        return copy(y_out.at[away], x_out.at[away, 1], y_sem, (away,), y_peer)

    def x_copy(away, ahead):
        return copy(
            x_out.at[away, :, ahead], x_in.at[away, ahead - 1], x_sem, (away, ahead - 1), x_peers[ahead - 1]
        )

    def z_copy(side, hop, part):
        piece = pl.ds(part * half, half)
        return copy(
            z_out.at[side, hop, piece], z_in.at[side, hop, piece], z_sem, (side, hop, part), z_peers[side]
        )

    group = 4

    def flatten(index, carry):
        values = pixels_ref[pl.ds(index * group, group)].astype(jnp.float32).reshape(group * WIN, 2 * LANES)
        at = pl.ds(pl.multiple_of(index * group * WIN, group * WIN), group * WIN)
        flat[0, at, :] = values[:, :LANES]
        flat[1, at, :] = values[:, LANES:]
        return carry

    lax.fori_loop(0, CHAN // group, flatten, 0, unroll=3)
    for part in range(2):
        flat[part, CHAN * WIN :, :] = jnp.zeros(((ROWS_PAD - CHAN) * WIN, LANES), jnp.float32)

    def row_block(part, block, row):
        return flat[part, pl.ds(block * 8 * WIN + row, 8, stride=WIN), :]

    def fill_halo(block, carry):
        at = pl.ds(pl.multiple_of(block * 8, 8), 8)
        for row in range(SHIFT):
            values = jnp.concatenate([row_block(0, block, row), row_block(1, block, row)], axis=1)
            halo_out[row, at, :] = values.astype(jnp.bfloat16)
        return carry

    lax.fori_loop(0, blocks, fill_halo, 0)
    pl.semaphore_wait(barrier, len(greeted))
    halo_copy().start()

    qkv_t[...] = lax.dot_general(
        head_columns(3 * HEADS), qkv_ref[...], (((1,), (1,)), ((), ())), preferred_element_type=jnp.float32
    ).astype(jnp.bfloat16)
    proj_t[...] = lax.dot_general(
        proj_ref[...], head_columns(HEADS), (((0,), (1,)), ((), ())), preferred_element_type=jnp.float32
    ).astype(jnp.bfloat16)
    hidden_t[...] = hidden_ref[...].astype(jnp.float32).T.astype(jnp.bfloat16)
    for index, gain_ref in enumerate((gain_one_ref, gain_two_ref)):
        gains[index] = jnp.broadcast_to(gain_ref[...], (LANES, CHAN)).T
    build_bias(table_ref, bias)
    source = iota((LANES, LANES), 0)
    target = iota((LANES, LANES), 1)

    def sorted_lane(lane):
        return ((lane >> 3) & (WIN - 1)) * (TILE * WIN) + (lane >> 6) * WIN + (lane & (WIN - 1))

    to_window = jnp.where(source == sorted_lane(target), 1.0, 0.0).astype(jnp.bfloat16)
    to_rows = jnp.where(target == sorted_lane(source), 1.0, 0.0).astype(jnp.bfloat16)

    halo_copy().wait_recv()

    def cut(block, carry):
        at = pl.ds(pl.multiple_of(block * 8, 8), 8)
        sides = [[], []]
        for row in range(WIN):
            if row < WIN - SHIFT:
                first, second = row_block(0, block, row + SHIFT), row_block(1, block, row + SHIFT)
            else:
                values = halo_in[row - WIN + SHIFT, at, :].astype(jnp.float32)
                first, second = values[:, :LANES], values[:, LANES:]
            first, second = shift_lanes(first, second, -SHIFT)
            sides[0].append(first)
            sides[1].append(second)
        for side in range(2):
            for index, values in enumerate(swap_blocks(sides[side])):
                mixed[side * 8 + index, at, :] = values
        return carry

    lax.fori_loop(0, blocks, cut, 0)

    def settle(tile, carry):
        natural[tile] = jnp.dot(
            mixed[tile].astype(jnp.bfloat16), to_window, preferred_element_type=jnp.float32
        )
        return carry

    lax.fori_loop(0, tiles, settle, 0, unroll=2)
    natural[tiles] = jnp.zeros((ROWS_PAD, LANES), jnp.float32)

    edge = CHAN - CHAN % 8
    edge_row = iota((ROWS_PAD - edge, LANES), 0) - (CHAN - edge)
    low = iota((ROWS_PAD, LANES), 1) < TOKENS
    low_edge = iota((ROWS_PAD - edge, LANES), 1) < TOKENS
    last_band = jnp.where(me == bands - 1, 1.0, 0.0)

    def finish_tile(values, slot, last_row, last_col):
        notes = jnp.where(edge_row == 0, slot, jnp.where(edge_row == 1, last_row, last_col))
        return jnp.concatenate(
            [values[:edge], jnp.where(edge_row < 0, values[edge:], notes)], axis=0
        ).astype(jnp.bfloat16)

    def pack(tile, carry):
        one = order_ref[tile * TILE]
        two = order_ref[tile * TILE + 1]
        first = natural[one >> 1]
        second = natural[two >> 1]
        first = jnp.where((one & 1) == 1, pltpu.roll(first, TOKENS, 1), first)
        second = jnp.where((two & 1) == 1, second, pltpu.roll(second, TOKENS, 1))
        last_col = jnp.where(
            low_edge,
            jnp.where(one == window_total - 1, 1.0, 0.0),
            jnp.where(two == window_total - 1, 1.0, 0.0),
        )
        packed[tile] = finish_tile(
            jnp.where(low, first, second), slot_ref[tile].astype(jnp.float32), last_band, last_col
        )
        return carry

    lax.fori_loop(0, tiles, pack, 0)
    packed[tiles] = finish_tile(natural[tiles], float(CAP), 0.0, 0.0)

    def stage(away):
        def step(ahead, carry):
            y_out[away, ahead] = packed[held_ref[band_of(x + ahead, z + away, y + 1)]]
            x_out[away, 0, ahead] = packed[held_ref[band_of(x + ahead, z + away, y)]]
            return carry

        lax.fori_loop(0, X_SIZE, step, 0)

    for away in order:
        stage(away)
        y_copy(away).start()

    def pass_x(away):
        y_copy(away).wait_recv()
        for ahead in range(1, X_SIZE):
            x_copy(away, ahead).start()

    def wait_x(away):
        for ahead in range(1, X_SIZE):
            x_copy(away, ahead).wait_recv()

    def gather(away, part, target, arrived):
        found = [x_out.at[away, 0, 0], x_out.at[away, 1, 0]]
        for ahead in range(X_SIZE - 1):
            found += [x_in.at[away, ahead, 0], x_in.at[away, ahead, 1]]

        def step(index, carry):
            slot = part * half + index
            number = slot.astype(jnp.float32)
            sum_ = None if arrived is None else arrived[slot]
            for one in found:
                mark = one[CHAN : CHAN + 1, :].astype(jnp.float32)
                term = one[...] * jnp.where(mark == number, 1.0, 0.0).astype(jnp.bfloat16)
                sum_ = term if sum_ is None else sum_ + term
            target[slot] = sum_
            return carry

        lax.fori_loop(0, half, step, 0)

    fed = [0]
    gaps = list(UNITS)

    def work(count=None):
        start = fed[0]
        count = tiles - start if count is None else min(count, tiles - start)
        if count == 0:
            return

        def step(tile, carry):
            values = natural[tile][:CHAN]
            last = jnp.logical_and(tile == tiles - 1, iota((TOKENS, LANES), 1) >= TOKENS)
            mask = region_mask(jnp.where(me == bands - 1, 1, 0), jnp.where(last, 1, 0))
            state = attend_tile(values, mask, gains[0], qkv_t[...], proj_t[...], bias)
            done = feed_tile(state, gains[1], hidden_t[...], output_ref[...])
            chosen = jnp.where(low[:CHAN], active_ref[tile * TILE], active_ref[tile * TILE + 1])
            done = jnp.where(chosen == 1, done, values).astype(jnp.bfloat16)
            mixed[tile, 0:CHAN, :] = jnp.dot(done, to_rows, preferred_element_type=jnp.float32)
            return carry

        lax.fori_loop(start, start + count, step, 0)
        fed[0] = start + count

    def fill():
        work(gaps.pop(0))

    def hop_far():
        wait_x(far)
        for side in range(2):
            gather(far, side, z_out.at[side, 0], None)
            z_copy(side, 0, side).start()

    def hop(side, number):
        away = far - number if side == 0 else Z_SIZE - far + number
        wait_x(away)
        parts = (1 - side, side) if number == 1 else (0, 1)
        for part in parts:
            if number == 1 and part != side:
                arrived = None
            else:
                z_copy(side, number - 1, part).wait_recv()
                arrived = z_in.at[side, number - 1]
            gather(away, part, z_out.at[side, number], arrived)
            z_copy(side, number, part).start()

    pass_x(order[0])
    fill()
    pass_x(order[1])
    fill()
    hop_far()
    pass_x(order[2])
    fill()
    pass_x(order[3])
    hop(0, 1)
    fill()
    hop(1, 1)
    pass_x(order[4])
    fill()
    pass_x(order[5])
    hop(0, 2)
    fill()
    hop(1, 2)
    pass_x(order[6])
    fill()
    pass_x(order[7])
    fill()
    hop(0, 3)
    fill()
    hop(1, 3)
    work()

    def join(block, carry):
        at = pl.ds(pl.multiple_of(block * 8, 8), 8)
        sides = [swap_blocks([mixed[side * 8 + index, at, :] for index in range(8)]) for side in range(2)]
        for row in range(WIN):
            first, second = shift_lanes(sides[0][row], sides[1][row], SHIFT)
            if row < WIN - SHIFT:
                place = pl.ds(block * 8 * WIN + row + SHIFT, 8, stride=WIN)
                flat[0, place, :] = first
                flat[1, place, :] = second
            else:
                values = jnp.concatenate([first, second], axis=1)
                rows_out[row - WIN + SHIFT, at, :] = values.astype(jnp.bfloat16)
        return carry

    lax.fori_loop(0, blocks, join, 0)
    rows_copy().start()
    wait_x(0)
    for part in range(2):
        gather(0, part, total_ref, None)
    for part in range(2):
        for side in range(2):
            z_copy(side, far - 1, part).wait_recv()

        def last_step(index, carry):
            slot = part * half + index
            values = total_ref[slot] + z_in[0, far - 1, slot] + z_in[1, far - 1, slot]
            values = values.astype(jnp.float32)
            last_row = values[CHAN + 1 : CHAN + 2]
            last_col = values[CHAN + 2 : CHAN + 3]
            mask = region_mask(jnp.where(last_row > 0, 1, 0), jnp.where(last_col > 0, 1, 0))
            state = attend_tile(values[:CHAN], mask, gains[0], qkv_t[...], proj_t[...], bias)
            done_ref[pl.ds(pl.multiple_of(slot * ROWS_PAD, 8), CHAN), :] = state.astype(jnp.float32)
            return carry

        lax.fori_loop(0, half, last_step, 0, unroll=2)

    def emit(index, carry):
        for inner in range(group):
            channel = index * group + inner
            work_ref[channel] = done_ref[pl.ds(channel, CAP, stride=ROWS_PAD), :].astype(jnp.bfloat16)
        return carry

    lax.fori_loop(0, CHAN // group, emit, 0)
    rows_copy().wait_recv()

    def take_rows(block, carry):
        at = pl.ds(pl.multiple_of(block * 8, 8), 8)
        for row in range(SHIFT):
            values = rows_in[row, at, :].astype(jnp.float32)
            place = pl.ds(block * 8 * WIN + row, 8, stride=WIN)
            flat[0, place, :] = values[:, :LANES]
            flat[1, place, :] = values[:, LANES:]
        return carry

    lax.fori_loop(0, blocks, take_rows, 0)

    def restore(index, carry):
        at = pl.ds(pl.multiple_of(index * group * WIN, group * WIN), group * WIN)
        values = jnp.concatenate([flat[0, at, :], flat[1, at, :]], axis=1)
        restored_ref[pl.ds(index * group, group)] = values.reshape(group, WIN, 2 * LANES).astype(jnp.bfloat16)
        return carry

    lax.fori_loop(0, CHAN // group, restore, 0, unroll=3)
    halo_copy().wait_send()
    rows_copy().wait_send()
    for away in order:
        y_copy(away).wait_send()
        for ahead in range(1, X_SIZE):
            x_copy(away, ahead).wait_send()
    for side in range(2):
        z_copy(side, 0, side).wait_send()
        for number in range(1, far):
            for part in range(2):
                z_copy(side, number, part).wait_send()


SMEM = pl.BlockSpec(memory_space=pltpu.SMEM)
VMEM = pl.BlockSpec(memory_space=pltpu.VMEM)


def shards(
    pixels,
    keep_mask,
    band_counts,
    plan_dest,
    plan_slot,
    bias_table,
    gain_attn,
    qkv_weight,
    proj_weight,
    gain_mlp,
    hidden_weight,
    output_weight,
):
    band_total = lax.axis_size("band")
    row_count, col_count, channels = pixels.shape
    window_total = keep_mask.shape[1]
    tile_total = window_total // TILE
    slots = plan_slot.reshape(-1)
    order, held, active = pl.pallas_call(
        plan_kernel,
        out_shape=[
            jax.ShapeDtypeStruct((window_total + 1,), jnp.int32),
            jax.ShapeDtypeStruct((band_total + 1,), jnp.int32),
            jax.ShapeDtypeStruct((window_total,), jnp.int32),
        ],
        in_specs=[SMEM] * 4,
        out_specs=[SMEM] * 3,
        name="plan",
    )(keep_mask.reshape(-1), band_counts, plan_dest.reshape(-1), slots)
    tile_shape = (ROWS_PAD, LANES)
    rows_shape = (SHIFT, ROWS_PAD, col_count)
    far = Z_SIZE // 2
    restored, work = pl.pallas_call(
        block_kernel,
        out_shape=[
            jax.ShapeDtypeStruct((channels, row_count, col_count), jnp.bfloat16),
            jax.ShapeDtypeStruct((channels, CAP, LANES), jnp.bfloat16),
        ],
        in_specs=[SMEM] * 4 + [VMEM] * 8,
        out_specs=[VMEM, VMEM],
        scratch_shapes=[
            pltpu.VMEM((2, ROWS_PAD * WIN, LANES), jnp.float32),
            pltpu.VMEM((tile_total,) + tile_shape, jnp.float32),
            pltpu.VMEM((tile_total + 1,) + tile_shape, jnp.float32),
            pltpu.VMEM((tile_total + 1,) + tile_shape, jnp.bfloat16),
            pltpu.VMEM((HEADS, TOKENS, LANES), jnp.float32),
            pltpu.VMEM((3 * HEADS * HEAD_PAD, CHAN), jnp.bfloat16),
            pltpu.VMEM((CHAN, HEADS * HEAD_PAD), jnp.bfloat16),
            pltpu.VMEM((FF_WIDTH, CHAN), jnp.bfloat16),
            pltpu.VMEM((2, CHAN, LANES), jnp.float32),
            pltpu.VMEM(rows_shape, jnp.bfloat16),
            pltpu.VMEM(rows_shape, jnp.bfloat16),
            pltpu.VMEM(rows_shape, jnp.bfloat16),
            pltpu.VMEM(rows_shape, jnp.bfloat16),
            pltpu.VMEM((Z_SIZE, X_SIZE) + tile_shape, jnp.bfloat16),
            pltpu.VMEM((Z_SIZE, Y_SIZE, X_SIZE) + tile_shape, jnp.bfloat16),
            pltpu.VMEM((Z_SIZE, X_SIZE - 1, Y_SIZE) + tile_shape, jnp.bfloat16),
            pltpu.VMEM((2, far, CAP) + tile_shape, jnp.bfloat16),
            pltpu.VMEM((2, far, CAP) + tile_shape, jnp.bfloat16),
            pltpu.VMEM((CAP,) + tile_shape, jnp.bfloat16),
            pltpu.VMEM((CAP * ROWS_PAD, LANES), jnp.float32),
            pltpu.SemaphoreType.DMA((2, 2)),
            pltpu.SemaphoreType.DMA((2, Z_SIZE)),
            pltpu.SemaphoreType.DMA((2, Z_SIZE, X_SIZE - 1)),
            pltpu.SemaphoreType.DMA((2, 2, far, 2)),
        ],
        compiler_params=pltpu.CompilerParams(
            vmem_limit_bytes=VMEM_LIMIT, collective_id=0, has_side_effects=True
        ),
        name="block",
    )(
        held,
        order,
        active,
        slots,
        jnp.transpose(pixels, (2, 0, 1)),
        bias_table.T,
        gain_attn.reshape(1, channels),
        qkv_weight,
        proj_weight,
        gain_mlp.reshape(1, channels),
        hidden_weight,
        output_weight.T,
    )
    return (jnp.transpose(restored, (1, 2, 0)), jnp.transpose(work, (1, 2, 0)))


def solution(mesh):
    sharded = P(("img", "band"))
    in_specs = (
        P(("img", "band"), None, None),
        P(("img", "band"), None),
        sharded,
        P(("img", "band"), None),
        P(("img", "band"), None),
    ) + (P(),) * 7
    out_specs = (P(("img", "band"), None, None), P(("img", "band"), None, None))
    return jax.shard_map(shards, mesh=mesh, in_specs=in_specs, out_specs=out_specs, check_vma=False)
```

time: 124 us -> 114 us (0.919); the launches traced: 123 us -> 114 us
  Pallas kernels: 95.3 us -> 110 us
  starting transfers between devices: 9.86 us -> 0 us
  local copies, waits for them, and re-layouts: 10.9 us -> 2.82 us
  waiting for transfers between devices: 3.14 us -> 0 us
  matrix products: 1.3 us -> 0 us
    pallas_call x2, Pallas kernels: 95.3 us -> 110 us  [the longest x1 108 us: shards(): pl.pallas_call(block_kernel, out_shape=[jax.ShapeDtypeStruct((channels, r...]
    ppermute x1 -> x0, starting transfers between devices: 9.86 us -> none  [from_behind(): return lax.ppermute(value, axis, pairs)]
    pallas_call x2 -> x0, local copies, waits for them, and re-layouts: 3.37 us -> none  [shards(): pl.pallas_call(exchange_kernel, out_shape=[jax.ShapeDtypeStruct((row_coun...]
    ppermute x1 -> x0, waiting for transfers between devices: 3.14 us -> none  [from_behind(): return lax.ppermute(value, axis, pairs)]
    transpose x3 -> x0, local copies, waits for them, and re-layouts: 2.13 us -> none  [the longest x1 0.75 us: shards(): jnp.pad(pad_heads(qkv_weight), ((0, pad), (0, 0)))]
    reshape x6 -> x0, local copies, waits for them, and re-layouts: 1.86 us -> none  [the longest x1 0.77 us: shards(): jnp.pad(gain_attn, (0, pad)).reshape(ROWS_PAD, 1)]
    dot_general x1 -> x0, matrix products: 1.3 us -> none  [position_bias(): lax.dot_general(bias_table, onehot, (((0,), (0,)), ((), ())), precision=l...]
    unnamed x23 -> x4, local copies, waits for them, and re-layouts: 2.67 us -> 2.82 us
  transfers between devices with their start and end apart: 1 -> 0, of which waited for: 1 -> 0; matrix products, arithmetic and copies ran while one was open for 6% -> 0% of each run, Pallas kernels for 0% -> 0%
where the time goes in v3:
time: 114 us
  Pallas kernels  110 us (96%)
  local copies, waits for them, and re-layouts  2.82 us (2%)
  between operations  1.3 us (1%)
    pallas_call x1, Pallas kernels, shards(): pl.pallas_call(block_kernel, out_shape=[jax.ShapeDtypeStruct((channels, r...  108 us
    unnamed x4, local copies, waits for them, and re-layouts  2.82 us

profile of v3, /device:TPU:8, one launch (start us, length us, event | category | flops | bytes accessed | tf_op | source)
XLA Modules:
  0.0 114.3 jit_solution(5570422754411670354)
XLA Ops:
  1.3 1.9 %plan.1 = (s32[33]{0:T(128)}, s32[65]{0:T(128)}, s32[32]{0:T(128)}) custom-call(s32[32]{0:T(128)} %bitcast.19, s32[1]{0:T(128)S(6)} %copy.16.count_ref, s32[16]{0:T(128)} %bitcast.20, s32[16]{0:T(128)} %bitcast.15), custom_call_target="tpu_custom_call" | custom-call | tf_op jit(solution)/shard_map/plan/pallas_call | solution.py:595
  3.1 108.4 %block.1 = (bf16[180,8,256]{2,1,0:T(8,128)(2,1)}, bf16[180,8,128]{2,1,0:T(8,128)(2,1)}) custom-call(s32[65]{0:T(128)} %get-tuple-element.7.held_ref, s32[33]{0:T(128)} %get-tuple-element.8.order_ref, s32[32]{0:T(128)} %get-tuple-element.9.active_ref, s32[16]{0:T(128)} %bitcast.16, bf16[180,8,256]{2,1,0:T(8,128)(2,1)} %bitcast.10, f32[6,225]{1,0:T(8,128)} %bitcast.14, ...), custom_call_target="tpu_custom_call" | custom-call | tf_op jit(solution)/shard_map/block/pallas_call | solution.py:609
  111.5 0.0 copy-start
  111.5 2.1 %copy.17 = bf16[8,256,180]{1,0,2:T(8,128)(2,1)} copy(bf16[8,256,180]{1,0,2:T(8,128)(2,1)} %bitcast.11) | data formatting | bytes 1474560
  113.6 0.0 copy-done
  113.6 0.7 copy.18
Async XLA Ops:
  111.5 2.1 %copy-start = (bf16[180,8,128]{2,1,0:T(8,128)(2,1)S(1)}, bf16[180,8,128]{2,1,0:T(8,128)(2,1)}, u32[]{:S(2)}) copy-start(bf16[180,8,128]{2,1,0:T(8,128)(2,1)} %get-tuple-element.11) | copy-start | bytes 1105924

commit v4 on v3

--- a/solution.py
+++ b/solution.py
@@ -14,6 +14,7 @@
 TOKENS = WIN * WIN
 TILE = 2
 LANES = TILE * TOKENS
+WIDE = 2 * LANES
 SHIFT = 4
 CAP = 8
 ROWS_PAD = 184
@@ -25,6 +26,10 @@
 VMEM_LIMIT = 60 << 20
 
 
+def iota(shape, dim):
+    return lax.broadcasted_iota(jnp.int32, shape, dim)
+
+
 def norm_columns(values, gain):
     center = values - jnp.sum(values, axis=0, keepdims=True) * (1.0 / CHAN)
     spread = jnp.sum(center * center, axis=0, keepdims=True) * (1.0 / CHAN)
@@ -37,41 +42,65 @@
     return high, low
 
 
-def attend_tile(x_cols, mask, gain, qkv_t, proj_t, bias_ref):
-    lane = lax.broadcasted_iota(jnp.int32, (TOKENS, LANES), 1)
-    first = lane < TOKENS
+def attend_pair(x_cols, mask, gain, qkv_t, proj_t, bias_ref):
+    low = (iota((TOKENS, WIDE), 1) & TOKENS) == 0
+    low_head = (iota((HEAD_PAD, WIDE), 1) & TOKENS) == 0
     normed = norm_columns(x_cols, gain)
     qkv = jnp.dot(qkv_t, normed, preferred_element_type=jnp.float32)
+    width = HEADS * HEAD_PAD
+    none = jnp.zeros((3 * HEAD_PAD, LANES), jnp.bfloat16)
     mixed = []
-    width = HEADS * HEAD_PAD
     for head in range(HEADS):
         at = head * HEAD_PAD
         query = qkv[at : at + HEAD_PAD] * HEAD_DIM ** (-0.5)
         key = qkv[width + at : width + at + HEAD_PAD]
-        value = qkv[2 * width + at : 2 * width + at + HEAD_PAD].astype(jnp.bfloat16)
+        value = qkv[2 * width + at : 2 * width + at + HEAD_PAD]
         query_high, query_low = split_two(query)
         key_high, key_low = split_two(key)
         left = jnp.concatenate([key_high, key_low, key_high], axis=0)
+        left = jnp.concatenate([left[:, :LANES], left[:, LANES:]], axis=0)
         right = jnp.concatenate([query_high, query_high, query_low], axis=0)
+        right = jnp.concatenate(
+            [
+                jnp.concatenate([right[:, :LANES], none], axis=1),
+                jnp.concatenate([none, right[:, LANES:]], axis=1),
+            ],
+            axis=0,
+        )
         full = lax.dot_general(
             left, right, (((0,), (0,)), ((), ())), preferred_element_type=jnp.float32
         )
-        scores = jnp.where(first, full[:TOKENS], full[TOKENS:])
-        scores = (scores + bias_ref[head]) + mask
+        scores = jnp.where(low, full[:TOKENS], full[TOKENS:])
+        line = bias_ref[head]
+        scores = (scores + jnp.concatenate([line, line], axis=1)) + mask
         top = jnp.max(scores, axis=0, keepdims=True)
         grown = jnp.exp(scores - top)
         total = jnp.sum(grown, axis=0, keepdims=True)
-        weights = grown * (1.0 / total)
-        spread = jnp.concatenate(
-            [jnp.where(first, weights, 0.0), jnp.where(first, 0.0, weights)], axis=0
-        ).astype(jnp.bfloat16)
-        mixed.append(jnp.dot(value, spread, preferred_element_type=jnp.float32).astype(jnp.bfloat16))
+        weights = (grown * (1.0 / total)).astype(jnp.bfloat16)
+        parts = []
+        for side in range(2):
+            part = value[:, side * LANES : (side + 1) * LANES]
+            parts += [part, pltpu.roll(part, TOKENS, 1)]
+        values = jnp.concatenate(parts, axis=0).astype(jnp.bfloat16)[:, :TOKENS]
+        sums = jnp.dot(values, weights, preferred_element_type=jnp.float32)
+        sides = []
+        for side in range(2):
+            base = 2 * side * HEAD_PAD
+            lanes = slice(side * LANES, (side + 1) * LANES)
+            sides.append(
+                jnp.where(
+                    low_head[:, lanes],
+                    sums[base : base + HEAD_PAD, lanes],
+                    sums[base + HEAD_PAD : base + 2 * HEAD_PAD, lanes],
+                )
+            )
+        mixed.append(jnp.concatenate(sides, axis=1).astype(jnp.bfloat16))
     mixed = jnp.concatenate(mixed, axis=0)
     projected = jnp.dot(proj_t, mixed, preferred_element_type=jnp.float32)
     return (x_cols + projected).astype(jnp.bfloat16)
 
 
-def feed_tile(state, gain, hidden_t, output_t):
+def feed_pair(state, gain, hidden_t, output_t):
     state = state.astype(jnp.float32)
     normed = norm_columns(state, gain)
     hidden = jnp.dot(hidden_t, normed, preferred_element_type=jnp.float32)
@@ -79,13 +108,9 @@
     return state + jnp.dot(output_t, inner, preferred_element_type=jnp.float32)
 
 
-def iota(shape, dim):
-    return lax.broadcasted_iota(jnp.int32, shape, dim)
-
-
 def region_mask(rows_split, cols_split):
-    key = iota((TOKENS, LANES), 0)
-    query = iota((TOKENS, LANES), 1) & (TOKENS - 1)
+    key = iota((TOKENS, WIDE), 0)
+    query = iota((TOKENS, WIDE), 1) & (TOKENS - 1)
     rows_differ = ((key ^ query) & (SHIFT * WIN)) != 0
     cols_differ = ((key ^ query) & SHIFT) != 0
     row_part = jnp.where(rows_differ, rows_split, 0)
@@ -140,13 +165,6 @@
     return blocks
 
 
-def shift_lanes(first, second, steps):
-    lane = iota(first.shape, 1)
-    first, second = pltpu.roll(first, steps % LANES, 1), pltpu.roll(second, steps % LANES, 1)
-    own = lane >= steps if steps > 0 else lane < LANES + steps
-    return jnp.where(own, first, second), jnp.where(own, second, first)
-
-
 def plan_kernel(keep_ref, count_ref, dest_ref, slot_ref, order_ref, held_ref, active_ref):
     total = active_ref.shape[0]
     bands = held_ref.shape[0] - 1
@@ -173,11 +191,16 @@
     lax.fori_loop(0, tiles, tile_step, 0)
 
 
+def aligned(value):
+    return value if isinstance(value, int) else pl.multiple_of(value, 8)
+
+
 def band_of(x, z, y):
     return (lax.rem(x, X_SIZE) * Z_SIZE + lax.rem(z, Z_SIZE)) * Y_SIZE + lax.rem(y, Y_SIZE)
 
 
-UNITS = (2, 1, 1, 2, 2, 2, 2, 2, 2)
+BLOCKS_AT_ONCE = 2
+UNITS = (1, 0, 1, 1, 1, 1, 1, 1, 1)
 
 
 def block_kernel(
@@ -312,19 +335,20 @@
     for index, gain_ref in enumerate((gain_one_ref, gain_two_ref)):
         gains[index] = jnp.broadcast_to(gain_ref[...], (LANES, CHAN)).T
     build_bias(table_ref, bias)
-    source = iota((LANES, LANES), 0)
-    target = iota((LANES, LANES), 1)
-
-    def sorted_lane(lane):
-        return ((lane >> 3) & (WIN - 1)) * (TILE * WIN) + (lane >> 6) * WIN + (lane & (WIN - 1))
-
-    to_window = jnp.where(source == sorted_lane(target), 1.0, 0.0).astype(jnp.bfloat16)
-    to_rows = jnp.where(target == sorted_lane(source), 1.0, 0.0).astype(jnp.bfloat16)
+    source = iota((WIDE, LANES), 0)
+    target = iota((WIDE, LANES), 1)
+    place = (target >> 6) * WIN + (target & (WIN - 1)) + SHIFT
+    found = ((target >> 3) & (WIN - 1)) * (TILE * WIN) + (place & 15) + (place >> 4) * LANES
+    to_window = jnp.where(source == found, 1.0, 0.0).astype(jnp.bfloat16)
+    place = ((target & 15) + TILE * WIN - SHIFT) & 15
+    found = jnp.where((target & 15) < SHIFT, 0, LANES) + (place >> 3) * TOKENS
+    found = found + (target >> 4) * WIN + (place & (WIN - 1))
+    to_rows = jnp.where(source == found, 1.0, 0.0).astype(jnp.bfloat16)
 
     halo_copy().wait_recv()
 
     def cut(block, carry):
-        at = pl.ds(pl.multiple_of(block * 8, 8), 8)
+        at = pl.ds(aligned(block * 8), 8)
         sides = [[], []]
         for row in range(WIN):
             if row < WIN - SHIFT:
@@ -332,7 +356,6 @@
             else:
                 values = halo_in[row - WIN + SHIFT, at, :].astype(jnp.float32)
                 first, second = values[:, :LANES], values[:, LANES:]
-            first, second = shift_lanes(first, second, -SHIFT)
             sides[0].append(first)
             sides[1].append(second)
         for side in range(2):
@@ -340,11 +363,23 @@
                 mixed[side * 8 + index, at, :] = values
         return carry
 
-    lax.fori_loop(0, blocks, cut, 0)
+    def each_block(step):
+        def body(index, carry):
+            for inner in range(BLOCKS_AT_ONCE):
+                step(index * BLOCKS_AT_ONCE + inner, 0)
+            return carry
+
+        whole = blocks // BLOCKS_AT_ONCE
+        lax.fori_loop(0, whole, body, 0)
+        for block in range(whole * BLOCKS_AT_ONCE, blocks):
+            step(block, 0)
+
+    each_block(cut)
 
     def settle(tile, carry):
+        both = jnp.concatenate([mixed[tile], mixed[lax.rem(tile + 1, tiles)]], axis=1)
         natural[tile] = jnp.dot(
-            mixed[tile].astype(jnp.bfloat16), to_window, preferred_element_type=jnp.float32
+            both.astype(jnp.bfloat16), to_window, preferred_element_type=jnp.float32
         )
         return carry
 
@@ -425,21 +460,28 @@
     fed = [0]
     gaps = list(UNITS)
 
+    pairs = tiles // 2
+    gain_one = jnp.concatenate([gains[0], gains[0]], axis=1)
+    gain_two = jnp.concatenate([gains[1], gains[1]], axis=1)
+    wide_low = iota((CHAN, LANES), 1) < TOKENS
+
     def work(count=None):
         start = fed[0]
-        count = tiles - start if count is None else min(count, tiles - start)
+        count = pairs - start if count is None else min(count, pairs - start)
         if count == 0:
             return
 
-        def step(tile, carry):
-            values = natural[tile][:CHAN]
-            last = jnp.logical_and(tile == tiles - 1, iota((TOKENS, LANES), 1) >= TOKENS)
+        def step(pair, carry):
+            values = jnp.concatenate([natural[pair * 2][:CHAN], natural[pair * 2 + 1][:CHAN]], axis=1)
+            last = jnp.logical_and(pair == pairs - 1, iota((TOKENS, WIDE), 1) >= WIDE - TOKENS)
             mask = region_mask(jnp.where(me == bands - 1, 1, 0), jnp.where(last, 1, 0))
-            state = attend_tile(values, mask, gains[0], qkv_t[...], proj_t[...], bias)
-            done = feed_tile(state, gains[1], hidden_t[...], output_ref[...])
-            chosen = jnp.where(low[:CHAN], active_ref[tile * TILE], active_ref[tile * TILE + 1])
-            done = jnp.where(chosen == 1, done, values).astype(jnp.bfloat16)
-            mixed[tile, 0:CHAN, :] = jnp.dot(done, to_rows, preferred_element_type=jnp.float32)
+            state = attend_pair(values, mask, gain_one, qkv_t[...], proj_t[...], bias)
+            done = feed_pair(state, gain_two, hidden_t[...], output_ref[...])
+            for side in range(2):
+                tile = pair * 2 + side
+                lanes = slice(side * LANES, (side + 1) * LANES)
+                chosen = jnp.where(wide_low, active_ref[tile * TILE], active_ref[tile * TILE + 1])
+                mixed[tile, 0:CHAN, :] = jnp.where(chosen == 1, done[:, lanes], values[:, lanes])
             return carry
 
         lax.fori_loop(start, start + count, step, 0)
@@ -493,11 +535,18 @@
     hop(1, 3)
     work()
 
+    def unsettle(tile, carry):
+        both = jnp.concatenate([mixed[lax.rem(tile + tiles - 1, tiles)], mixed[tile]], axis=1)
+        natural[tile] = jnp.dot(both.astype(jnp.bfloat16), to_rows, preferred_element_type=jnp.float32)
+        return carry
+
+    lax.fori_loop(0, tiles, unsettle, 0, unroll=2)
+
     def join(block, carry):
-        at = pl.ds(pl.multiple_of(block * 8, 8), 8)
-        sides = [swap_blocks([mixed[side * 8 + index, at, :] for index in range(8)]) for side in range(2)]
+        at = pl.ds(aligned(block * 8), 8)
+        sides = [swap_blocks([natural[side * 8 + index, at, :] for index in range(8)]) for side in range(2)]
         for row in range(WIN):
-            first, second = shift_lanes(sides[0][row], sides[1][row], SHIFT)
+            first, second = sides[0][row], sides[1][row]
             if row < WIN - SHIFT:
                 place = pl.ds(block * 8 * WIN + row + SHIFT, 8, stride=WIN)
                 flat[0, place, :] = first
@@ -507,7 +556,7 @@
                 rows_out[row - WIN + SHIFT, at, :] = values.astype(jnp.bfloat16)
         return carry
 
-    lax.fori_loop(0, blocks, join, 0)
+    each_block(join)
     rows_copy().start()
     wait_x(0)
     for part in range(2):
@@ -517,17 +566,24 @@
             z_copy(side, far - 1, part).wait_recv()
 
         def last_step(index, carry):
-            slot = part * half + index
-            values = total_ref[slot] + z_in[0, far - 1, slot] + z_in[1, far - 1, slot]
-            values = values.astype(jnp.float32)
+            two = []
+            for side in range(2):
+                slot = part * half + index * 2 + side
+                values = total_ref[slot] + z_in[0, far - 1, slot] + z_in[1, far - 1, slot]
+                two.append(values.astype(jnp.float32))
+            values = jnp.concatenate(two, axis=1)
             last_row = values[CHAN + 1 : CHAN + 2]
             last_col = values[CHAN + 2 : CHAN + 3]
             mask = region_mask(jnp.where(last_row > 0, 1, 0), jnp.where(last_col > 0, 1, 0))
-            state = attend_tile(values[:CHAN], mask, gains[0], qkv_t[...], proj_t[...], bias)
-            done_ref[pl.ds(pl.multiple_of(slot * ROWS_PAD, 8), CHAN), :] = state.astype(jnp.float32)
+            state = attend_pair(values[:CHAN], mask, gain_one, qkv_t[...], proj_t[...], bias)
+            state = state.astype(jnp.float32)
+            for side in range(2):
+                slot = part * half + index * 2 + side
+                lanes = slice(side * LANES, (side + 1) * LANES)
+                done_ref[pl.ds(pl.multiple_of(slot * ROWS_PAD, 8), CHAN), :] = state[:, lanes]
             return carry
 
-        lax.fori_loop(0, half, last_step, 0, unroll=2)
+        lax.fori_loop(0, half // 2, last_step, 0)
 
     def emit(index, carry):
         for inner in range(group):

time: 114 us -> 91.3 us (0.80)
  Pallas kernels: 110 us -> 86.4 us
    pallas_call x1, Pallas kernels: 108 us -> 84.5 us  [shards(): pl.pallas_call(block_kernel, out_shape=[jax.ShapeDtypeStruct((channels, r...]
where the time goes in v4:
time: 91.3 us; the launch traced here: 90.5 us
  Pallas kernels  86.4 us (95%)
  local copies, waits for them, and re-layouts  2.82 us (3%)
  between operations  1.3 us (1%)
    pallas_call x1, Pallas kernels, shards(): pl.pallas_call(block_kernel, out_shape=[jax.ShapeDtypeStruct((channels, r...  84.5 us
    unnamed x4, local copies, waits for them, and re-layouts  2.82 us
    pallas_call x1, Pallas kernels, shards(): pl.pallas_call(plan_kernel, out_shape=[jax.ShapeDtypeStruct((window_total...  1.86 us

profile of v4, /device:TPU:8, one launch (start us, length us, event | category | flops | bytes accessed | tf_op | source)
XLA Modules:
  0.0 90.5 jit_solution(7687397653506725502)
XLA Ops:
  1.3 1.9 %plan.1 = (s32[33]{0:T(128)}, s32[65]{0:T(128)}, s32[32]{0:T(128)}) custom-call(s32[32]{0:T(128)} %bitcast.19, s32[1]{0:T(128)S(6)} %copy.16.count_ref, s32[16]{0:T(128)} %bitcast.20, s32[16]{0:T(128)} %bitcast.15), custom_call_target="tpu_custom_call" | custom-call | tf_op jit(solution)/shard_map/plan/pallas_call | solution.py:651
  3.1 84.5 %block.1 = (bf16[180,8,256]{2,1,0:T(8,128)(2,1)}, bf16[180,8,128]{2,1,0:T(8,128)(2,1)}) custom-call(s32[65]{0:T(128)} %get-tuple-element.7.held_ref, s32[33]{0:T(128)} %get-tuple-element.8.order_ref, s32[32]{0:T(128)} %get-tuple-element.9.active_ref, s32[16]{0:T(128)} %bitcast.16, bf16[180,8,256]{2,1,0:T(8,128)(2,1)} %bitcast.10, f32[6,225]{1,0:T(8,128)} %bitcast.14, ...), custom_call_target="tpu_custom_call" | custom-call | tf_op jit(solution)/shard_map/block/pallas_call | solution.py:665
  87.7 0.0 copy-start
  87.7 2.1 %copy.17 = bf16[8,256,180]{1,0,2:T(8,128)(2,1)} copy(bf16[8,256,180]{1,0,2:T(8,128)(2,1)} %bitcast.11) | data formatting | bytes 1474560
  89.8 0.0 copy-done
  89.8 0.7 copy.18
Async XLA Ops:
  87.7 2.1 %copy-start = (bf16[180,8,128]{2,1,0:T(8,128)(2,1)S(1)}, bf16[180,8,128]{2,1,0:T(8,128)(2,1)}, u32[]{:S(2)}) copy-start(bf16[180,8,128]{2,1,0:T(8,128)(2,1)} %get-tuple-element.11) | copy-start | bytes 1105924

commit v5 on v4

--- a/solution.py
+++ b/solution.py
@@ -165,7 +165,20 @@
     return blocks
 
 
-def plan_kernel(keep_ref, count_ref, dest_ref, slot_ref, order_ref, held_ref, active_ref):
+def hop_order():
+    far = Z_SIZE // 2
+    order = [far]
+    for away in range(far - 1, 0, -1):
+        order += [away, Z_SIZE - away]
+    return order + [0]
+
+
+def position():
+    me = lax.axis_index("band")
+    return me // (Z_SIZE * Y_SIZE), lax.rem(me // Y_SIZE, Z_SIZE), lax.rem(me, Y_SIZE)
+
+
+def plan_kernel(keep_ref, count_ref, dest_ref, slot_ref, order_ref, held_ref, active_ref, list_ref, place_ref):
     total = active_ref.shape[0]
     bands = held_ref.shape[0] - 1
     tiles = dest_ref.shape[0]
@@ -190,6 +203,18 @@
 
     lax.fori_loop(0, tiles, tile_step, 0)
 
+    x, z, y = position()
+    for index in range(tiles + 1):
+        list_ref[index] = tiles
+    count = jnp.int32(0)
+    for away in hop_order():
+        for ahead in range(X_SIZE):
+            tile = held_ref[band_of(x + ahead, z + away, y + 1)]
+            live = tile < tiles
+            list_ref[jnp.where(live, count, tiles)] = tile
+            place_ref[away * X_SIZE + ahead] = jnp.where(live, count, tiles)
+            count = count + live.astype(jnp.int32)
+
 
 def aligned(value):
     return value if isinstance(value, int) else pl.multiple_of(value, 8)
@@ -199,15 +224,19 @@
     return (lax.rem(x, X_SIZE) * Z_SIZE + lax.rem(z, Z_SIZE)) * Y_SIZE + lax.rem(y, Y_SIZE)
 
 
-BLOCKS_AT_ONCE = 2
-UNITS = (1, 0, 1, 1, 1, 1, 1, 1, 1)
+BLOCKS_AT_ONCE = 4
+X_ORDER = (2, 1, 3)
+OWN_FIRST = 3
+UNITS = (2, 1, 1, 1, 1, 1, 1)
 
 
 def block_kernel(
     held_ref,
     order_ref,
     active_ref,
+    list_ref,
     slot_ref,
+    place_ref,
     pixels_ref,
     table_ref,
     gain_one_ref,
@@ -231,13 +260,21 @@
     halo_in,
     rows_out,
     rows_in,
+    place_in,
+    places,
     y_out,
+    y_in_one,
+    y_in_two,
+    y_in_three,
+    y_in_four,
     x_out,
     x_in,
     z_out,
     z_in,
     total_ref,
     done_ref,
+    place_sem,
+    halo_sem,
     rows_sem,
     y_sem,
     x_sem,
@@ -245,9 +282,7 @@
 ):
     me = lax.axis_index("band")
     bands = lax.axis_size("band")
-    x = me // (Z_SIZE * Y_SIZE)
-    z = lax.rem(me // Y_SIZE, Z_SIZE)
-    y = lax.rem(me, Y_SIZE)
+    x, z, y = position()
     x_peers = [band_of(x + step, z, y) for step in range(1, X_SIZE)]
     y_peer = band_of(x, z, y + 1)
     z_peers = [band_of(x, z + 1, y), band_of(x, z + Z_SIZE - 1, y)]
@@ -263,10 +298,7 @@
     window_total = active_ref.shape[0]
     half = CAP // 2
     far = Z_SIZE // 2
-    order = [far]
-    for away in range(far - 1, 0, -1):
-        order += [away, Z_SIZE - away]
-    order += [0]
+    order = hop_order()
 
     def copy(source, target, sems, index, peer):
         return pltpu.make_async_remote_copy(
@@ -278,18 +310,30 @@
             device_id_type=MESH,
         )
 
-    def halo_copy():
-        return copy(halo_out, halo_in, rows_sem, (0,), before)
+    def halo_copy(side):
+        lanes = pl.ds(side * LANES, LANES)
+        return copy(halo_out.at[:, :, lanes], halo_in.at[:, :, lanes], halo_sem, (side,), before)
 
     def rows_copy():
         return copy(rows_out, rows_in, rows_sem, (1,), after)
 
-    def y_copy(away):
-        return copy(y_out.at[away], x_out.at[away, 1], y_sem, (away,), y_peer)
-
-    def x_copy(away, ahead):
+    y_ins = (y_in_one, y_in_two, y_in_three, y_in_four)
+    y_piece = tiles // len(y_ins)
+
+    def y_copy(index):
+        piece = pl.ds(index * y_piece, y_piece)
+        return copy(y_out.at[piece], y_ins[index].at[pl.ds(0, y_piece)], y_sem, (index,), y_peer)
+
+    def place_copy():
+        return copy(place_ref, place_in, rows_sem, (0,), y_peer)
+
+    def x_copy(away, ahead, who):
         return copy(
-            x_out.at[away, :, ahead], x_in.at[away, ahead - 1], x_sem, (away, ahead - 1), x_peers[ahead - 1]
+            x_out.at[away, who, ahead],
+            x_in.at[away, ahead - 1, who],
+            x_sem,
+            (away, ahead - 1, who),
+            x_peers[ahead - 1],
         )
 
     def z_copy(side, hop, part):
@@ -323,7 +367,9 @@
 
     lax.fori_loop(0, blocks, fill_halo, 0)
     pl.semaphore_wait(barrier, len(greeted))
-    halo_copy().start()
+    place_copy().start()
+    for side in range(2):
+        halo_copy(side).start()
 
     qkv_t[...] = lax.dot_general(
         head_columns(3 * HEADS), qkv_ref[...], (((1,), (1,)), ((), ())), preferred_element_type=jnp.float32
@@ -345,23 +391,13 @@
     found = found + (target >> 4) * WIN + (place & (WIN - 1))
     to_rows = jnp.where(source == found, 1.0, 0.0).astype(jnp.bfloat16)
 
-    halo_copy().wait_recv()
-
-    def cut(block, carry):
+    def cut(side, block):
         at = pl.ds(aligned(block * 8), 8)
-        sides = [[], []]
-        for row in range(WIN):
-            if row < WIN - SHIFT:
-                first, second = row_block(0, block, row + SHIFT), row_block(1, block, row + SHIFT)
-            else:
-                values = halo_in[row - WIN + SHIFT, at, :].astype(jnp.float32)
-                first, second = values[:, :LANES], values[:, LANES:]
-            sides[0].append(first)
-            sides[1].append(second)
-        for side in range(2):
-            for index, values in enumerate(swap_blocks(sides[side])):
-                mixed[side * 8 + index, at, :] = values
-        return carry
+        lanes = slice(side * LANES, (side + 1) * LANES)
+        lines = [row_block(side, block, row + SHIFT) for row in range(WIN - SHIFT)]
+        lines += [halo_in[row, at, lanes].astype(jnp.float32) for row in range(SHIFT)]
+        for index, values in enumerate(swap_blocks(lines)):
+            mixed[side * 8 + index, at, :] = values
 
     def each_block(step):
         def body(index, carry):
@@ -374,7 +410,9 @@
         for block in range(whole * BLOCKS_AT_ONCE, blocks):
             step(block, 0)
 
-    each_block(cut)
+    for side in range(2):
+        halo_copy(side).wait_recv()
+        each_block(lambda block, carry, side=side: cut(side, block))
 
     def settle(tile, carry):
         both = jnp.concatenate([mixed[tile], mixed[lax.rem(tile + 1, tiles)]], axis=1)
@@ -383,7 +421,7 @@
         )
         return carry
 
-    lax.fori_loop(0, tiles, settle, 0, unroll=2)
+    lax.fori_loop(0, tiles, settle, 0, unroll=4)
     natural[tiles] = jnp.zeros((ROWS_PAD, LANES), jnp.float32)
 
     edge = CHAN - CHAN % 8
@@ -415,29 +453,61 @@
         )
         return carry
 
-    lax.fori_loop(0, tiles, pack, 0)
+    lax.fori_loop(0, tiles, pack, 0, unroll=2)
     packed[tiles] = finish_tile(natural[tiles], float(CAP), 0.0, 0.0)
 
-    def stage(away):
+    for y_in in y_ins:
+        y_in[y_piece] = jnp.zeros((ROWS_PAD, LANES), jnp.bfloat16)
+
+    def list_step(index, carry):
+        y_out[index] = packed[list_ref[index]]
+        return carry
+
+    def own_x(away):
         def step(ahead, carry):
-            y_out[away, ahead] = packed[held_ref[band_of(x + ahead, z + away, y + 1)]]
             x_out[away, 0, ahead] = packed[held_ref[band_of(x + ahead, z + away, y)]]
             return carry
 
         lax.fori_loop(0, X_SIZE, step, 0)
-
-    for away in order:
-        stage(away)
-        y_copy(away).start()
-
-    def pass_x(away):
-        y_copy(away).wait_recv()
-        for ahead in range(1, X_SIZE):
-            x_copy(away, ahead).start()
+        for ahead in X_ORDER:
+            x_copy(away, ahead, 0).start()
+
+    for index in range(4):
+        lax.fori_loop(index * y_piece, (index + 1) * y_piece, list_step, 0)
+        y_copy(index).start()
+        if index < OWN_FIRST:
+            own_x(order[index])
+    place_copy().wait_recv()
+    kept = pltpu.make_async_copy(place_in, places, place_sem)
+    kept.start()
+    kept.wait()
+
+    def pass_x(index):
+        away = order[index]
+        if index < 4:
+            y_copy(index).wait_recv()
+
+        def step(ahead, carry):
+            place = places[away * X_SIZE + ahead]
+            found = None
+            for piece in range(min(index + 1, len(y_ins))):
+                within = place - piece * y_piece
+                hit = jnp.logical_and(within >= 0, within < y_piece)
+                one = y_ins[piece][jnp.where(hit, within, y_piece)]
+                found = one if found is None else found + one
+            x_out[away, 1, ahead] = found
+            return carry
+
+        lax.fori_loop(0, X_SIZE, step, 0)
+        for ahead in X_ORDER:
+            x_copy(away, ahead, 1).start()
+        if index + OWN_FIRST < len(order):
+            own_x(order[index + OWN_FIRST])
 
     def wait_x(away):
-        for ahead in range(1, X_SIZE):
-            x_copy(away, ahead).wait_recv()
+        for ahead in X_ORDER:
+            for who in range(Y_SIZE):
+                x_copy(away, ahead, who).wait_recv()
 
     def gather(away, part, target, arrived):
         found = [x_out.at[away, 0, 0], x_out.at[away, 1, 0]]
@@ -509,38 +579,34 @@
             gather(away, part, z_out.at[side, number], arrived)
             z_copy(side, number, part).start()
 
-    pass_x(order[0])
+    pass_x(0)
     fill()
-    pass_x(order[1])
+    pass_x(1)
     fill()
     hop_far()
-    pass_x(order[2])
+    pass_x(2)
     fill()
-    pass_x(order[3])
+    pass_x(3)
+    fill()
     hop(0, 1)
     fill()
     hop(1, 1)
-    pass_x(order[4])
+    pass_x(4)
     fill()
-    pass_x(order[5])
+    pass_x(5)
     hop(0, 2)
     fill()
     hop(1, 2)
-    pass_x(order[6])
-    fill()
-    pass_x(order[7])
-    fill()
-    hop(0, 3)
-    fill()
-    hop(1, 3)
+    pass_x(6)
     work()
+    pass_x(7)
 
     def unsettle(tile, carry):
         both = jnp.concatenate([mixed[lax.rem(tile + tiles - 1, tiles)], mixed[tile]], axis=1)
         natural[tile] = jnp.dot(both.astype(jnp.bfloat16), to_rows, preferred_element_type=jnp.float32)
         return carry
 
-    lax.fori_loop(0, tiles, unsettle, 0, unroll=2)
+    lax.fori_loop(0, tiles, unsettle, 0, unroll=4)
 
     def join(block, carry):
         at = pl.ds(aligned(block * 8), 8)
@@ -558,9 +624,31 @@
 
     each_block(join)
     rows_copy().start()
+    hop(0, 3)
+    hop(1, 3)
     wait_x(0)
     for part in range(2):
         gather(0, part, total_ref, None)
+    rows_copy().wait_recv()
+
+    def take_rows(block, carry):
+        at = pl.ds(pl.multiple_of(block * 8, 8), 8)
+        for row in range(SHIFT):
+            values = rows_in[row, at, :].astype(jnp.float32)
+            place = pl.ds(block * 8 * WIN + row, 8, stride=WIN)
+            flat[0, place, :] = values[:, :LANES]
+            flat[1, place, :] = values[:, LANES:]
+        return carry
+
+    lax.fori_loop(0, blocks, take_rows, 0)
+
+    def restore(index, carry):
+        at = pl.ds(pl.multiple_of(index * group * WIN, group * WIN), group * WIN)
+        values = jnp.concatenate([flat[0, at, :], flat[1, at, :]], axis=1)
+        restored_ref[pl.ds(index * group, group)] = values.reshape(group, WIN, 2 * LANES).astype(jnp.bfloat16)
+        return carry
+
+    lax.fori_loop(0, CHAN // group, restore, 0, unroll=3)
     for part in range(2):
         for side in range(2):
             z_copy(side, far - 1, part).wait_recv()
@@ -592,32 +680,16 @@
         return carry
 
     lax.fori_loop(0, CHAN // group, emit, 0)
-    rows_copy().wait_recv()
-
-    def take_rows(block, carry):
-        at = pl.ds(pl.multiple_of(block * 8, 8), 8)
-        for row in range(SHIFT):
-            values = rows_in[row, at, :].astype(jnp.float32)
-            place = pl.ds(block * 8 * WIN + row, 8, stride=WIN)
-            flat[0, place, :] = values[:, :LANES]
-            flat[1, place, :] = values[:, LANES:]
-        return carry
-
-    lax.fori_loop(0, blocks, take_rows, 0)
-
-    def restore(index, carry):
-        at = pl.ds(pl.multiple_of(index * group * WIN, group * WIN), group * WIN)
-        values = jnp.concatenate([flat[0, at, :], flat[1, at, :]], axis=1)
-        restored_ref[pl.ds(index * group, group)] = values.reshape(group, WIN, 2 * LANES).astype(jnp.bfloat16)
-        return carry
-
-    lax.fori_loop(0, CHAN // group, restore, 0, unroll=3)
-    halo_copy().wait_send()
+    for side in range(2):
+        halo_copy(side).wait_send()
     rows_copy().wait_send()
+    place_copy().wait_send()
+    for index in range(4):
+        y_copy(index).wait_send()
     for away in order:
-        y_copy(away).wait_send()
-        for ahead in range(1, X_SIZE):
-            x_copy(away, ahead).wait_send()
+        for ahead in X_ORDER:
+            for who in range(Y_SIZE):
+                x_copy(away, ahead, who).wait_send()
     for side in range(2):
         z_copy(side, 0, side).wait_send()
         for number in range(1, far):
@@ -648,15 +720,17 @@
     window_total = keep_mask.shape[1]
     tile_total = window_total // TILE
     slots = plan_slot.reshape(-1)
-    order, held, active = pl.pallas_call(
+    order, held, active, listed, place = pl.pallas_call(
         plan_kernel,
         out_shape=[
             jax.ShapeDtypeStruct((window_total + 1,), jnp.int32),
             jax.ShapeDtypeStruct((band_total + 1,), jnp.int32),
             jax.ShapeDtypeStruct((window_total,), jnp.int32),
+            jax.ShapeDtypeStruct((tile_total + 1,), jnp.int32),
+            jax.ShapeDtypeStruct((LANES,), jnp.int32),
         ],
         in_specs=[SMEM] * 4,
-        out_specs=[SMEM] * 3,
+        out_specs=[SMEM] * 5,
         name="plan",
     )(keep_mask.reshape(-1), band_counts, plan_dest.reshape(-1), slots)
     tile_shape = (ROWS_PAD, LANES)
@@ -668,7 +742,7 @@
             jax.ShapeDtypeStruct((channels, row_count, col_count), jnp.bfloat16),
             jax.ShapeDtypeStruct((channels, CAP, LANES), jnp.bfloat16),
         ],
-        in_specs=[SMEM] * 4 + [VMEM] * 8,
+        in_specs=[SMEM] * 5 + [VMEM] * 9,
         out_specs=[VMEM, VMEM],
         scratch_shapes=[
             pltpu.VMEM((2, ROWS_PAD * WIN, LANES), jnp.float32),
@@ -684,16 +758,24 @@
             pltpu.VMEM(rows_shape, jnp.bfloat16),
             pltpu.VMEM(rows_shape, jnp.bfloat16),
             pltpu.VMEM(rows_shape, jnp.bfloat16),
-            pltpu.VMEM((Z_SIZE, X_SIZE) + tile_shape, jnp.bfloat16),
+            pltpu.VMEM((LANES,), jnp.int32),
+            pltpu.SMEM((LANES,), jnp.int32),
+            pltpu.VMEM((tile_total,) + tile_shape, jnp.bfloat16),
+            pltpu.VMEM((tile_total // 4 + 1,) + tile_shape, jnp.bfloat16),
+            pltpu.VMEM((tile_total // 4 + 1,) + tile_shape, jnp.bfloat16),
+            pltpu.VMEM((tile_total // 4 + 1,) + tile_shape, jnp.bfloat16),
+            pltpu.VMEM((tile_total // 4 + 1,) + tile_shape, jnp.bfloat16),
             pltpu.VMEM((Z_SIZE, Y_SIZE, X_SIZE) + tile_shape, jnp.bfloat16),
             pltpu.VMEM((Z_SIZE, X_SIZE - 1, Y_SIZE) + tile_shape, jnp.bfloat16),
             pltpu.VMEM((2, far, CAP) + tile_shape, jnp.bfloat16),
             pltpu.VMEM((2, far, CAP) + tile_shape, jnp.bfloat16),
             pltpu.VMEM((CAP,) + tile_shape, jnp.bfloat16),
             pltpu.VMEM((CAP * ROWS_PAD, LANES), jnp.float32),
+            pltpu.SemaphoreType.DMA(()),
             pltpu.SemaphoreType.DMA((2, 2)),
-            pltpu.SemaphoreType.DMA((2, Z_SIZE)),
-            pltpu.SemaphoreType.DMA((2, Z_SIZE, X_SIZE - 1)),
+            pltpu.SemaphoreType.DMA((2, 2)),
+            pltpu.SemaphoreType.DMA((2, 4)),
+            pltpu.SemaphoreType.DMA((2, Z_SIZE, X_SIZE - 1, Y_SIZE)),
             pltpu.SemaphoreType.DMA((2, 2, far, 2)),
         ],
         compiler_params=pltpu.CompilerParams(
@@ -704,7 +786,9 @@
         held,
         order,
         active,
+        listed,
         slots,
+        place,
         jnp.transpose(pixels, (2, 0, 1)),
         bias_table.T,
         gain_attn.reshape(1, channels),

time: 91.3 us -> 88 us (0.964)
  Pallas kernels: 86.4 us -> 82.8 us
    pallas_call x1, Pallas kernels: 84.5 us -> 80.8 us  [shards(): pl.pallas_call(block_kernel, out_shape=[jax.ShapeDtypeStruct((channels, r...]
where the time goes in v5:
time: 88 us; the launch traced here: 86.9 us
  Pallas kernels  82.8 us (94%)
  local copies, waits for them, and re-layouts  2.82 us (3%)
  between operations  1.3 us (1%)
    pallas_call x1, Pallas kernels, shards(): pl.pallas_call(block_kernel, out_shape=[jax.ShapeDtypeStruct((channels, r...  80.8 us
    unnamed x4, local copies, waits for them, and re-layouts  2.82 us
    pallas_call x1, Pallas kernels, shards(): pl.pallas_call(plan_kernel, out_shape=[jax.ShapeDtypeStruct((window_total...  2.02 us

profile of v5, /device:TPU:8, one launch (start us, length us, event | category | flops | bytes accessed | tf_op | source)
XLA Modules:
  0.0 86.9 jit_solution(16480674595821269735)
XLA Ops:
  1.3 2.0 %plan.1 = (s32[33]{0:T(128)}, s32[65]{0:T(128)}, s32[32]{0:T(128)}, s32[17]{0:T(128)}, s32[128]{0:T(128)}) custom-call(s32[32]{0:T(128)} %bitcast.19, s32[1]{0:T(128)S(6)} %copy.16.count_ref, s32[16]{0:T(128)} %bitcast.20, s32[16]{0:T(128)} %bitcast.15), custom_call_target="tpu_custom_call" | custom-call | tf_op jit(solution)/shard_map/plan/pallas_call | solution.py:723
  3.3 80.8 %block.1 = (bf16[180,8,256]{2,1,0:T(8,128)(2,1)}, bf16[180,8,128]{2,1,0:T(8,128)(2,1)}) custom-call(s32[65]{0:T(128)} %get-tuple-element.9.held_ref, s32[33]{0:T(128)} %get-tuple-element.10.order_ref, s32[32]{0:T(128)} %get-tuple-element.11.active_ref, s32[17]{0:T(128)} %get-tuple-element.12.list_ref, s32[16]{0:T(128)} %bitcast.16, ...), custom_call_target="tpu_custom_call" | custom-call | tf_op jit(solution)/shard_map/block/pallas_call | solution.py:739
  84.1 0.0 copy-start
  84.1 2.1 %copy.17 = bf16[8,256,180]{1,0,2:T(8,128)(2,1)} copy(bf16[8,256,180]{1,0,2:T(8,128)(2,1)} %bitcast.11) | data formatting | bytes 1474560
  86.2 0.0 copy-done
  86.2 0.7 copy.18
Async XLA Ops:
  84.1 2.1 %copy-start = (bf16[180,8,128]{2,1,0:T(8,128)(2,1)S(1)}, bf16[180,8,128]{2,1,0:T(8,128)(2,1)}, u32[]{:S(2)}) copy-start(bf16[180,8,128]{2,1,0:T(8,128)(2,1)} %get-tuple-element.15) | copy-start | bytes 1105924

commit v6 on v5

--- a/solution.py
+++ b/solution.py
@@ -453,7 +453,7 @@
         )
         return carry
 
-    lax.fori_loop(0, tiles, pack, 0, unroll=2)
+    lax.fori_loop(0, tiles, pack, 0, unroll=4)
     packed[tiles] = finish_tile(natural[tiles], float(CAP), 0.0, 0.0)
 
     for y_in in y_ins:
@@ -525,7 +525,7 @@
             target[slot] = sum_
             return carry
 
-        lax.fori_loop(0, half, step, 0)
+        lax.fori_loop(0, half, step, 0, unroll=2)
 
     fed = [0]
     gaps = list(UNITS)
@@ -671,7 +671,7 @@
                 done_ref[pl.ds(pl.multiple_of(slot * ROWS_PAD, 8), CHAN), :] = state[:, lanes]
             return carry
 
-        lax.fori_loop(0, half // 2, last_step, 0)
+        lax.fori_loop(0, half // 2, last_step, 0, unroll=2)
 
     def emit(index, carry):
         for inner in range(group):
@@ -679,7 +679,7 @@
             work_ref[channel] = done_ref[pl.ds(channel, CAP, stride=ROWS_PAD), :].astype(jnp.bfloat16)
         return carry
 
-    lax.fori_loop(0, CHAN // group, emit, 0)
+    lax.fori_loop(0, CHAN // group, emit, 0, unroll=3)
     for side in range(2):
         halo_copy(side).wait_send()
     rows_copy().wait_send()

time: 88 us -> 86.4 us (0.982)
  Pallas kernels: 82.8 us -> 81.2 us
    pallas_call x1, Pallas kernels: 80.8 us -> 79.2 us  [shards(): pl.pallas_call(block_kernel, out_shape=[jax.ShapeDtypeStruct((channels, r...]
where the time goes in v6:
time: 86.4 us; the launch traced here: 85.3 us
  Pallas kernels  81.2 us (94%)
  local copies, waits for them, and re-layouts  2.82 us (3%)
  between operations  1.3 us (2%)
    pallas_call x1, Pallas kernels, shards(): pl.pallas_call(block_kernel, out_shape=[jax.ShapeDtypeStruct((channels, r...  79.2 us
    unnamed x4, local copies, waits for them, and re-layouts  2.82 us
    pallas_call x1, Pallas kernels, shards(): pl.pallas_call(plan_kernel, out_shape=[jax.ShapeDtypeStruct((window_total...  2.02 us

profile of v6, /device:TPU:8, one launch (start us, length us, event | category | flops | bytes accessed | tf_op | source)
XLA Modules:
  0.0 85.3 jit_solution(3291633342698053136)
XLA Ops:
  1.3 2.0 %plan.1 = (s32[33]{0:T(128)}, s32[65]{0:T(128)}, s32[32]{0:T(128)}, s32[17]{0:T(128)}, s32[128]{0:T(128)}) custom-call(s32[32]{0:T(128)} %bitcast.19, s32[1]{0:T(128)S(6)} %copy.16.count_ref, s32[16]{0:T(128)} %bitcast.20, s32[16]{0:T(128)} %bitcast.15), custom_call_target="tpu_custom_call" | custom-call | tf_op jit(solution)/shard_map/plan/pallas_call | solution.py:723
  3.3 79.2 %block.1 = (bf16[180,8,256]{2,1,0:T(8,128)(2,1)}, bf16[180,8,128]{2,1,0:T(8,128)(2,1)}) custom-call(s32[65]{0:T(128)} %get-tuple-element.9.held_ref, s32[33]{0:T(128)} %get-tuple-element.10.order_ref, s32[32]{0:T(128)} %get-tuple-element.11.active_ref, s32[17]{0:T(128)} %get-tuple-element.12.list_ref, s32[16]{0:T(128)} %bitcast.16, ...), custom_call_target="tpu_custom_call" | custom-call | tf_op jit(solution)/shard_map/block/pallas_call | solution.py:739
  82.5 0.0 copy-start
  82.5 2.1 %copy.17 = bf16[8,256,180]{1,0,2:T(8,128)(2,1)} copy(bf16[8,256,180]{1,0,2:T(8,128)(2,1)} %bitcast.11) | data formatting | bytes 1474560
  84.6 0.0 copy-done
  84.6 0.7 copy.18
Async XLA Ops:
  82.5 2.1 %copy-start = (bf16[180,8,128]{2,1,0:T(8,128)(2,1)S(1)}, bf16[180,8,128]{2,1,0:T(8,128)(2,1)}, u32[]{:S(2)}) copy-start(bf16[180,8,128]{2,1,0:T(8,128)(2,1)} %get-tuple-element.15) | copy-start | bytes 1105924
